TPU v7x, 128 devices: a whole 4x4x4 slice. The times are simulated.
128 devices in a mesh: dp: 2 (over y_lo), section: 4 (over z), mp: 16 (over x, y_hi, core).
Axes of the slice: x: 4, y: 4 (y_hi: 2, y_lo: 2; y = y_hi * 2 + y_lo), z: 4, core: 2. Of those that a mesh axis runs over, the one named last changes fastest.
Arguments:
- token_ids: int32 [32, 32], P('dp'), may hold values from 0 to 65535
- members: int32 [32], replicated, may hold values from 0 to 31, each once
- owners: int32 [4], replicated, may hold values from 0 to 3, each once
- embed_table: bfloat16 [4096, 65536], P('mp', 'section'), may hold values from -6 to 6
- norm_gain: float32 [4, 4096], P('section'), may hold values from 0.5 to 2
- gate_weight: bfloat16 [4, 4096, 10240], P('section', None, 'mp'), may hold values from -0.09375 to 0.09375
- up_weight: bfloat16 [4, 4096, 10240], P('section', None, 'mp'), may hold values from -0.09375 to 0.09375
- down_weight: bfloat16 [4, 4096, 10240], P('section', None, 'mp'), may hold values from -0.078125 to 0.078125
- final_gain: float32 [4096], replicated, may hold values from 0.5 to 2
- head_weight: bfloat16 [4096, 4096], P(None, 'mp'), may hold values from -0.0014648438 to 0.0014648438
Outputs:
- wins: float32 [4, 8, 8], P('dp', 'section')
Inputs may be any that keep to these rules, and one draw needn't show every extreme that they name: Prompt p's responses are members[8 * p] to members[8 * p + 7]; each response belongs to one prompt. `owners`: each slot holds one prompt.
All inputs are finite; a program needn't handle non-finite values.
Results may differ from a plain program's by a relative error of at most 0.028.
Values may be sent and summed in bfloat16 or wider, within the bound.
No kernel may reach another device: no remote copies, remote signals or barrier semaphores. Data moves between devices by JAX's collectives and lax.ppermute only.
A program may use at most 128 MiB of HBM per device.

v0:
```python
import functools

import jax
import jax.numpy as jnp
from jax import lax
from jax.experimental import pallas as pl
from jax.experimental.pallas import tpu as pltpu
from jax.sharding import PartitionSpec as P

GROUP = 8
BLOCKS = 2
AXES = ("dp", "section", "mp")

norm_eps = 1e-05
final_eps = 1e-06
bf16 = jnp.bfloat16
f32 = jnp.float32


def moved(value, target):
    pairs = []
    for dp in range(2):
        for z in range(4):
            for x in range(4):
                for y in range(2):
                    for c in range(2):
                        to = target(dp, z, x, y, c)
                        if to is not None:
                            d, s, a, b, e = to
                            pairs.append(
                                (dp * 64 + z * 16 + x * 4 + y * 2 + c, d * 64 + s * 16 + a * 4 + b * 2 + e)
                            )
    return lax.ppermute(value, AXES, pairs)


def along_x(value, shift):
    return moved(value, lambda d, z, x, y, c: (d, z, (x + shift) % 4, y, c))


def other_core(value):
    return moved(value, lambda d, z, x, y, c: (d, z, x, y, 1 - c))


def other_dp(value):
    return moved(value, lambda d, z, x, y, c: (1 - d, z, x, y, c))


def other_y(value):
    return moved(value, lambda d, z, x, y, c: (1 - d, z, x, 1 - y, c))


def to_first(value, source):
    return moved(value, lambda d, z, x, y, c: (d, 0, x, y, c) if z == source else None)


def onward(value, flip):
    return moved(value, lambda d, z, x, y, c: (d ^ flip, z + 1, x, y ^ flip, c) if z < 3 else None)


def nt_dot(a, b):
    return lax.dot_general(a, b, (((1,), (1,)), ((), ())), preferred_element_type=f32)


def embed_kernel(width, ids_ref, table_ref, *refs):
    outs, (held, sems) = refs[:-2], refs[-2:]
    rows = ids_ref.shape[0]
    steps = table_ref.shape[1] // width

    def copy(step):
        cols = pl.ds(pl.multiple_of(step * width, width), width)
        return pltpu.make_async_copy(table_ref.at[:, cols], held.at[:, cols], sems.at[step])

    def begin(step, carry):
        copy(step).start()
        return carry

    lax.fori_loop(0, steps, begin, 0)

    def one(step, acc):
        copy(step).wait()
        start = pl.multiple_of(step * width, width)
        hot = lax.broadcasted_iota(jnp.int32, (rows, width), 1) == ids_ref[...] - start
        return acc + nt_dot(hot.astype(f32).astype(bf16), held[:, pl.ds(start, width)])

    acc = lax.fori_loop(0, steps, one, jnp.zeros((rows, table_ref.shape[0]), f32))
    count = rows // len(outs)
    for i, out in enumerate(outs):
        out[...] = acc[i * count : (i + 1) * count].astype(bf16)


def in_hbm(value):
    return pltpu.with_memory_space_constraint(value, pltpu.HBM)


def in_vmem(value):
    return pltpu.with_memory_space_constraint(value, pltpu.VMEM)


VMEM_SPEC = pl.BlockSpec(memory_space=pltpu.VMEM)
HBM_SPEC = pl.BlockSpec(memory_space=pltpu.HBM)
SMEM_SPEC = pl.BlockSpec(memory_space=pltpu.SMEM)


def embed_parts(ids, table, count):
    width = 1024
    rows = ids.shape[0] // count
    return pl.pallas_call(
        functools.partial(embed_kernel, width),
        in_specs=[VMEM_SPEC, HBM_SPEC],
        out_specs=[VMEM_SPEC] * count,
        out_shape=[pltpu.VMEM((rows, table.shape[0]), bf16)] * count,
        scratch_shapes=[
            pltpu.VMEM(table.shape, bf16),
            pltpu.SemaphoreType.DMA((table.shape[1] // width,)),
        ],
        compiler_params=pltpu.CompilerParams(vmem_limit_bytes=24 * 1024 * 1024),
        name="embed",
    )(in_vmem(ids), in_hbm(table))


def load_kernel(count, after, *refs):
    sources, places, sems = refs[:count], refs[count : 2 * count], refs[-1]
    copies = []
    for i, (source, place) in enumerate(zip(sources, places)):
        rows = source.shape[1] // 4
        for k in range(4):
            where = (0, pl.ds(k * rows, rows))
            copies.append(
                pltpu.make_async_copy(source.at[where], place.at[where], sems.at[4 * i + k])
            )
    for copy in copies:
        copy.start()
    for copy in copies:
        copy.wait()


def loaded(after, *arrays):
    count = len(arrays)
    return pl.pallas_call(
        functools.partial(load_kernel, count),
        in_specs=[VMEM_SPEC] + [HBM_SPEC] * count,
        out_specs=[VMEM_SPEC] * count,
        out_shape=[pltpu.VMEM(a.shape, a.dtype) for a in arrays],
        scratch_shapes=[pltpu.SemaphoreType.DMA((4 * count,))],
        compiler_params=pltpu.CompilerParams(vmem_limit_bytes=1024 * 1024),
        name="load",
    )(in_vmem(after), *[in_hbm(a) for a in arrays])


def prepare(x, c, chunks, gain_ref, scaled_ref, inverse_ref):
    def one(step, carry):
        rows = pl.ds(pl.multiple_of(step * 32, 32), 32)
        squares = None
        for shift in range(4):
            base = lax.rem(x + 4 - shift, 4) * 1024
            for ref, core in ((chunks[shift], c), (chunks[4 + shift], 1 - c)):
                for y in range(2):
                    block = ref[rows, y * 256 : (y + 1) * 256].astype(f32)
                    off = pl.multiple_of(base + y * 512 + core * 256, 256)
                    scaled_ref[rows, pl.ds(off, 256)] = (
                        block * gain_ref[:, pl.ds(off, 256)]
                    ).astype(bf16)
                    part = block[:, :128] * block[:, :128] + block[:, 128:] * block[:, 128:]
                    squares = part if squares is None else squares + part
        total = jnp.sum(squares, axis=1, keepdims=True)
        inverse_ref[rows, :] = jnp.broadcast_to(lax.rsqrt(total / 4096 + norm_eps), (32, 128))
        return carry

    lax.fori_loop(0, chunks[0].shape[0] // 32, one, 0)


def hidden_units(scaled, wg, wu, inverse_ref, gate_ref, up_ref):
    def one(k, carry):
        cols = pl.ds(pl.multiple_of(k * 1024, 1024), 1024)
        part = scaled[:, cols]
        gate = jnp.dot(part, wg[0, cols, :], preferred_element_type=f32)
        up = jnp.dot(part, wu[0, cols, :], preferred_element_type=f32)
        gate_ref[...] = jnp.where(k == 0, gate, gate_ref[...] + gate)
        up_ref[...] = jnp.where(k == 0, up, up_ref[...] + up)
        return carry

    lax.fori_loop(0, 4, one, 0)
    inverse = inverse_ref[:, :1]
    gate = gate_ref[...] * inverse
    return gate / (1.0 + jnp.exp(-gate)) * (up_ref[...] * inverse)


def mean_tokens(value):
    rows, cols = value.shape
    return jnp.sum(value.reshape(rows // 32, 32, cols), axis=1) * (1.0 / 32)


def mlp_kernel(pool, place, *refs):
    chunks, (gain, wg, wu, wd) = refs[:8], refs[8:12]
    send, keep = refs[12:14]
    scaled, inverse, gate, up = refs[-4:]
    x, c = place[0], place[1]
    prepare(x, c, chunks, gain, scaled, inverse)
    hidden = hidden_units(scaled, wg, wu, inverse, gate, up)
    if pool:
        refs[14][...] = mean_tokens(hidden)
        refs[15][...] = mean_tokens(chunks[0][...].astype(f32))
    rounded = hidden.astype(bf16)
    first = c == 0

    def one(s, carry):
        rows = pl.multiple_of(lax.rem(x + s, 4) * 1024, 1024)
        term = nt_dot(rounded, wd[0, pl.ds(rows, 1024), :])
        for y in range(2):
            a = term[:, y * 512 : y * 512 + 256]
            b = term[:, y * 512 + 256 : y * 512 + 512]
            cols = slice(y * 256, (y + 1) * 256)
            keep[s, :, cols] = jnp.where(first, a, b).astype(bf16)
            send[s, :, cols] = jnp.where(first, b, a).astype(bf16)
        return carry

    lax.fori_loop(0, 4, one, 0)


def last_kernel(count, place, *refs):
    chunks, (gain, wg, wu, wd) = refs[:8], refs[8:12]
    before = refs[12 : 12 + count]
    out, base = refs[12 + count : 14 + count]
    scaled, inverse, gate, up = refs[-4:]
    x, c = place[0], place[1]
    prepare(x, c, chunks, gain, scaled, inverse)
    hidden = hidden_units(scaled, wg, wu, inverse, gate, up)
    base[...] = mean_tokens(chunks[0][...].astype(f32))
    every = jnp.concatenate([ref[...] for ref in before] + [mean_tokens(hidden)], axis=0)
    high = every.astype(bf16)
    low = (every - high.astype(f32)).astype(bf16)
    rows = every.shape[0]
    stacked = jnp.concatenate([high, low], axis=0)

    def one(m, carry):
        term = nt_dot(stacked, wd[0, pl.ds(pl.multiple_of(m * 256, 256), 256), :])
        out[m] = term[:rows] + term[rows:]
        return carry

    lax.fori_loop(0, 16, one, 0)


def gathered_kernel(own, a, b, d, out):
    out[...] = (
        own[...].astype(f32) + a[...].astype(f32) + (b[...].astype(f32) + d[...].astype(f32))
    ).astype(bf16)


def by_y(flag, own, peer):
    first = flag[2] == 0
    low, high = own[...].astype(f32), peer[...].astype(f32)
    return jnp.concatenate(
        [jnp.where(first, low, high), jnp.where(first, high, low)], axis=1
    )


def fresh_kernel(flag, own, peer, out):
    out[...] = by_y(flag, own, peer).astype(bf16)


def halves_kernel(keep, got, own, *out):
    own[...] = keep[0].astype(f32) + got[0].astype(f32)
    for s in range(1, 4):
        out[s - 1][...] = (keep[s].astype(f32) + got[s].astype(f32)).astype(bf16)


def total_kernel(flag, own, state, a, b, d, out):
    base = jnp.where(flag[2] == 0, state[...].astype(f32), 0.0)
    out[...] = (
        own[...] + base + (a[...].astype(f32) + b[...].astype(f32) + d[...].astype(f32))
    ).astype(bf16)


def join_kernel(flag, a, b, out):
    out[...] = (a[...].astype(f32) + b[...].astype(f32)).astype(bf16)


def join_fresh_kernel(flag, a, b, own, peer, out):
    joined = a[...].astype(f32) + b[...].astype(f32)
    out[...] = jnp.where(flag[3] == 0, by_y(flag, own, peer), joined).astype(bf16)


def local(kernel, scalars, values, outs, scratch=(), name=None):
    single = not isinstance(outs, list)
    return pl.pallas_call(
        kernel,
        in_specs=[SMEM_SPEC] * len(scalars) + [VMEM_SPEC] * len(values),
        out_specs=VMEM_SPEC if single else [VMEM_SPEC] * len(outs),
        out_shape=outs,
        scratch_shapes=list(scratch),
        compiler_params=pltpu.CompilerParams(vmem_limit_bytes=20 * 1024 * 1024),
        name=name,
    )(*scalars, *[in_vmem(v) for v in values])


def out_vmem(shape, dtype):
    return pltpu.VMEM(shape, dtype)


def mlp_scratch(tokens):
    return [
        pltpu.VMEM((tokens, 4096), bf16),
        pltpu.VMEM((tokens, 128), f32),
        pltpu.VMEM((tokens, 640), f32),
        pltpu.VMEM((tokens, 640), f32),
    ]


def call_mlp(place, mine, theirs, gain, weights, pool):
    tokens = mine[0].shape[0]
    outs = [out_vmem((4, tokens, 512), bf16)] * 2
    if pool:
        outs += [out_vmem((tokens // 32, 640), f32), out_vmem((tokens // 32, 512), f32)]
    return local(
        functools.partial(mlp_kernel, pool), [place], [*mine, *theirs, gain, *weights], outs,
        mlp_scratch(tokens), "mlp",
    )


def call_last(place, mine, theirs, gain, weights, before):
    tokens = mine[0].shape[0]
    rows = sum(b.shape[0] for b in before) + tokens // 32
    return local(
        functools.partial(last_kernel, len(before)), [place],
        [*mine, *theirs, gain, *weights, *before],
        [out_vmem((16, rows, 256), f32), out_vmem((tokens // 32, 512), f32)],
        mlp_scratch(tokens), "last_mlp",
    )


def head_kernel(place, chosen_ref, all_ref, gain_ref, head_ref, out_ref):
    total = squares = None
    for m in range(16):
        cols = slice(m * 256, (m + 1) * 256)
        side = (m // 2) % 2
        v = jnp.concatenate([all_ref[side, m], all_ref[1 - side, m]], axis=0)
        now = jnp.dot(v, head_ref[cols, :], preferred_element_type=f32)
        total = now if total is None else total + now
        plain = v.astype(f32) / gain_ref[:, cols]
        plain = plain * plain
        plain = plain[:, :128] + plain[:, 128:]
        squares = plain if squares is None else squares + plain
    factor = lax.rsqrt(jnp.sum(squares, axis=1, keepdims=True) / 4096 + final_eps)
    here = place[0]
    side = lax.rem(here // 2, 2)
    mine = jnp.concatenate([all_ref[side, here], all_ref[1 - side, here]], axis=0)
    mine = mine.astype(f32) * factor
    scores = lax.dot_general(
        total * factor, mine, (((1,), (1,)), ((), ())),
        precision=lax.Precision.HIGHEST, preferred_element_type=f32,
    )
    skew = scores - scores.T
    chosen = chosen_ref[...]
    count = skew.shape[0]
    hot = (lax.broadcasted_iota(jnp.int32, (chosen.shape[0], count), 1) == chosen).astype(f32)
    rows = jnp.dot(hot, skew, precision=lax.Precision.HIGHEST, preferred_element_type=f32)
    out_ref[...] = lax.dot_general(
        rows, hot, (((1,), (1,)), ((), ())),
        precision=lax.Precision.HIGHEST, preferred_element_type=f32,
    )


def head_part(place, chosen, everyone, gain, head):
    vmem = pl.BlockSpec(memory_space=pltpu.VMEM)
    return pl.pallas_call(
        head_kernel,
        in_specs=[pl.BlockSpec(memory_space=pltpu.SMEM)] + [vmem] * 4,
        out_specs=vmem,
        out_shape=jax.ShapeDtypeStruct((chosen.shape[0], chosen.shape[0]), f32),
        name="head",
    )(place, chosen, everyone, gain, head)


def per_device(
    token_ids, members, owners, embed_table, norm_gain, gate_weight, up_weight, down_weight,
    final_gain, head_weight,
):
    section = lax.axis_index("section")
    mp = lax.axis_index("mp")
    dp = lax.axis_index("dp")
    x, y, c = mp // 4, (mp // 2) % 2, mp % 2
    place = jnp.stack([x, c, y, section]).astype(jnp.int32)
    ids = jnp.where(y == 0, token_ids, other_dp(token_ids))
    flat = ids.reshape(-1, 1) - section * embed_table.shape[1]
    parts = embed_parts(flat, embed_table, BLOCKS)
    weights = loaded(parts[0], gate_weight, up_weight, down_weight)
    size = (parts[0].shape[0], 512)
    half = (parts[0].shape[0], 256)

    fresh = []
    for part in parts:
        pieces = [to_first(part, z) for z in (1, 3, 2)]
        own = local(gathered_kernel, [], [part, *pieces], out_vmem(half, bf16), (), "gathered")
        fresh.append((own, other_y(own)))
    state = local(fresh_kernel, [place], fresh[0], out_vmem(size, bf16), (), "fresh")
    sums_state, sums_hidden = [], []
    ticks = BLOCKS + 3
    for tick in range(ticks):
        mine = [state] + [along_x(state, s) for s in (1, 3, 2)]
        mine = [mine[i] for i in (0, 1, 3, 2)]
        theirs = [other_core(m) for m in mine]
        if tick == ticks - 1:
            terms, base = call_last(place, mine, theirs, norm_gain, weights, sums_hidden)
            sums_state.append(base)
            break
        send, keep, *pooled = call_mlp(place, mine, theirs, norm_gain, weights, tick >= 3)
        if tick >= 3:
            sums_hidden.append(pooled[0])
            sums_state.append(pooled[1])
        own, *halves = local(
            halves_kernel, [], [keep, other_core(send)],
            [out_vmem(size, f32)] + [out_vmem(size, bf16)] * 3, (), "halves",
        )
        arrived = [along_x(halves[s - 1], s) for s in (1, 3, 2)]
        total = local(
            total_kernel, [place], [own, state, *arrived], out_vmem(size, bf16), (), "total"
        )
        ahead = [onward(total, 0), onward(total, 1)]
        kernel = join_kernel
        if tick + 1 < BLOCKS:
            ahead += fresh[tick + 1]
            kernel = join_fresh_kernel
        state = local(kernel, [place], ahead, out_vmem(size, bf16), (), "join")

    groups = [[(g ^ ((m // 2) % 2)) * 16 + m for m in range(16)] for g in range(2)]
    pieces = lax.all_to_all(
        terms, ("dp", "mp"), 0, 0, tiled=True, axis_index_groups=groups
    )
    base = jnp.concatenate(sums_state, axis=0)
    pooled = jnp.sum(pieces, axis=0) + jnp.where(y == 0, base[:, :256], base[:, 256:])
    gain_here = lax.dynamic_slice_in_dim(final_gain, mp * 256, 256)
    value = (pooled * gain_here[None, :]).astype(bf16)
    everyone = lax.all_to_all(
        jnp.broadcast_to(value, (32, *value.shape)), ("dp", "mp"), 0, 0, tiled=True
    ).reshape(2, 16, *value.shape)

    prompts = owners.shape[0]
    here = prompts // 2
    slots = dp * here + jnp.arange(here, dtype=jnp.int32)
    match = (owners[None, :] == slots[:, None]).astype(jnp.int32)
    hit = match[:, :, None] * members.reshape(prompts, GROUP)[None]
    chosen = jnp.sum(hit, axis=1).reshape(here * GROUP, 1)
    tile = head_part(
        jnp.reshape(mp, (1,)).astype(jnp.int32), chosen, everyone, final_gain[None], head_weight
    )
    rows = GROUP // 4
    parts = jnp.stack(
        [tile[p * GROUP : (p + 1) * GROUP, p * GROUP : (p + 1) * GROUP] for p in range(here)]
    )
    parts = jnp.swapaxes(parts.reshape(here, 4, rows, GROUP), 0, 1).reshape(4, here * rows, GROUP)
    parts = jnp.pad(parts, ((0, 0), (0, 8 - here * rows), (0, 128 - GROUP)))
    parts = jnp.broadcast_to(parts[None, :, None], (2, 4, 16, 8, 128)).reshape(128, 8, 128)
    got = lax.all_to_all(parts, AXES, 0, 0, tiled=True).reshape(2, 4, 16, 8, 128)
    skew = jnp.sum(jnp.where(dp == 0, got[0, 3], got[1, 3]), axis=0)[: here * rows, :GROUP]
    return jax.nn.sigmoid(skew).reshape(here, rows, GROUP)


def solution(mesh):
    placed = (
        P("dp", None),
        P(),
        P(),
        P("mp", "section"),
        P("section", None),
        P("section", None, "mp"),
        P("section", None, "mp"),
        P("section", None, "mp"),
        P(),
        P(None, "mp"),
    )
    return jax.shard_map(
        per_device, mesh=mesh, in_specs=placed, out_specs=P("dp", "section", None), check_vma=False
    )
```

profile of v0, /device:TPU:0, one launch (start us, length us, event | category | flops | bytes accessed | tf_op | source)
XLA Modules:
  0.0 359.0 jit_solution(1362519414074791604)
XLA Ops:
  4.8 11.9 %embed.1 = (bf16[256,256]{1,0:T(8,128)(2,1)S(1)}, bf16[256,256]{1,0:T(8,128)(2,1)S(1)}) custom-call(s32[512,1]{1,0:T(8,128)S(1)} %sub.20.ids_ref, bf16[256,16384]{1,0:T(8,128)(2,1)} %table_ref.1), custom_call_target="tpu_custom_call" | custom-call | tf_op jit(solution)/shard_map/embed/pallas_call | solution.py:107
  20.7 3.0 collective-permute-done.1.a
  23.6 4.6 %collective-permute-done.2.b = bf16[256,256]{1,0:T(8,128)(2,1)S(1)} collective-permute-done((bf16[256,256]{1,0:T(8,128)(2,1)S(1)}, bf16[256,256]{1,0:T(8,128)(2,1)S(1)}, u32[]{:S(2)}, u32[]{:S(2)}) %collective-permute-start.2) | collective-permute-done | bytes 131104 | tf_op jit(solution)/shard_map/ppermute | solution.py:33
  30.9 3.6 %collective-permute-done.4.peer = bf16[256,256]{1,0:T(8,128)(2,1)S(1)} collective-permute-done((bf16[256,256]{1,0:T(8,128)(2,1)S(1)}, bf16[256,256]{1,0:T(8,128)(2,1)S(1)}, u32[]{:S(2)}, u32[]{:S(2)}) %collective-permute-start.4) | collective-permute-done | bytes 131104 | tf_op jit(solution)/shard_map/ppermute | solution.py:33
  35.1 3.3 collective-permute-start.6
  40.4 3.3 collective-permute-done.6.refs_2_
  43.8 3.0 collective-permute-done.7.refs_3_
  47.3 5.6 %load.1 = (bf16[1,4096,640]{2,1,0:T(8,128)(2,1)S(1)}, bf16[1,4096,640]{2,1,0:T(8,128)(2,1)S(1)}, bf16[1,4096,640]{2,1,0:T(8,128)(2,1)S(1)}) custom-call(bf16[256,256]{1,0:T(8,128)(2,1)S(1)} %get-tuple-element.38.own.after, bf16[1,4096,640]{2,1,0:T(8,128)(2,1)} %refs_0_.1, bf16[1,4096,640]{2,1,0:T(8,128)(2,1)} %refs_1_.1, bf16[1,4096,640]{2,1,0:T(8,128)(2,1)} %refs_2_.1), custom_call_target="tpu_custom_call" | custom-call | tf_op jit(solution)/shard_map/load/pallas_call | solution.py:139
  53.0 8.4 %mlp.4 = (bf16[4,256,512]{2,1,0:T(8,128)(2,1)S(1)}, bf16[4,256,512]{2,1,0:T(8,128)(2,1)S(1)}) custom-call(s32[4]{0:T(128)S(1)} %pad_add_fusion.flag.place, bf16[256,512]{1,0:T(8,128)(2,1)S(1)} %fresh.1.refs_0_.state, bf16[256,512]{1,0:T(8,128)(2,1)S(1)} %collective-permute-done.5.refs_1_, bf16[256,512]{1,0:T(8,128)(2,1)S(1)} %collective-permute-done.6.refs_2_, ...), custom_call_target="tpu_custom_call" | custom-call | tf_op jit(solution)/shard_map/mlp/pallas_call | solution.py:285
  71.6 2.9 collective-permute-done.13.a
  75.7 3.4 collective-permute-done.14.b
  82.5 4.0 %collective-permute-start.17 = (bf16[256,512]{1,0:T(8,128)(2,1)S(1)}, bf16[256,512]{1,0:T(8,128)(2,1)S(1)}, u32[]{:S(2)}, u32[]{:S(2)}) collective-permute-start(bf16[256,512]{1,0:T(8,128)(2,1)S(1)} %total.4), channel_id=1, source_target_pairs={{0,82},{1,83},{2,80},{3,81},{4,86},{5,87},{6,84},{7,85},{8,90},{9,... | collective-permute-start | bytes 786440 | tf_op jit(solution)/shard_map/ppermute | solution.py:33
  87.7 7.8 %collective-permute-done.21.peer = bf16[256,256]{1,0:T(8,128)(2,1)S(1)} collective-permute-done((bf16[256,256]{1,0:T(8,128)(2,1)S(1)}, bf16[256,256]{1,0:T(8,128)(2,1)S(1)}, u32[]{:S(2)}, u32[]{:S(2)}) %collective-permute-start.21) | collective-permute-done | bytes 131104 | tf_op jit(solution)/shard_map/ppermute | solution.py:33
  99.8 9.3 %collective-permute-done.22.refs_1_ = bf16[256,512]{1,0:T(8,128)(2,1)S(1)} collective-permute-done((bf16[256,512]{1,0:T(8,128)(2,1)S(1)}, bf16[256,512]{1,0:T(8,128)(2,1)S(1)}, u32[]{:S(2)}, u32[]{:S(2)}) %collective-permute-start.22) | collective-permute-done | bytes 262176 | tf_op jit(solution)/shard_map/ppermute | solution.py:33
  111.4 8.4 %mlp.5 = (bf16[4,256,512]{2,1,0:T(8,128)(2,1)S(1)}, bf16[4,256,512]{2,1,0:T(8,128)(2,1)S(1)}) custom-call(s32[4]{0:T(128)S(1)} %pad_add_fusion.flag.place, bf16[256,512]{1,0:T(8,128)(2,1)S(1)} %join.4.refs_0_.state, bf16[256,512]{1,0:T(8,128)(2,1)S(1)} %collective-permute-done.22.refs_1_, bf16[256,512]{1,0:T(8,128)(2,1)S(1)} %collective-permute-done.23.refs_2_, ...), custom_call_target="tpu_custom_call" | custom-call | tf_op jit(solution)/shard_map/mlp/pallas_call | solution.py:285
  123.1 3.0 collective-permute-start.31
  126.7 6.0 %collective-permute-done.30.a = bf16[256,512]{1,0:T(8,128)(2,1)S(1)} collective-permute-done((bf16[256,512]{1,0:T(8,128)(2,1)S(1)}, bf16[256,512]{1,0:T(8,128)(2,1)S(1)}, u32[]{:S(2)}, u32[]{:S(2)}) %collective-permute-start.30) | collective-permute-done | bytes 262176 | tf_op jit(solution)/shard_map/ppermute | solution.py:33
  132.7 4.6 %collective-permute-done.31.b = bf16[256,512]{1,0:T(8,128)(2,1)S(1)} collective-permute-done((bf16[256,512]{1,0:T(8,128)(2,1)S(1)}, bf16[256,512]{1,0:T(8,128)(2,1)S(1)}, u32[]{:S(2)}, u32[]{:S(2)}) %collective-permute-start.31) | collective-permute-done | bytes 262176 | tf_op jit(solution)/shard_map/ppermute | solution.py:33
  139.3 3.0 collective-permute-start.33
  142.4 3.7 %collective-permute-start.34 = (bf16[256,512]{1,0:T(8,128)(2,1)S(1)}, bf16[256,512]{1,0:T(8,128)(2,1)S(1)}, u32[]{:S(2)}, u32[]{:S(2)}) collective-permute-start(bf16[256,512]{1,0:T(8,128)(2,1)S(1)} %total.5), channel_id=1, source_target_pairs={{0,82},{1,83},{2,80},{3,81},{4,86},{5,87},{6,84},{7,85},{8,90},{9,... | collective-permute-start | bytes 786440 | tf_op jit(solution)/shard_map/ppermute | solution.py:33
  146.0 6.9 %collective-permute-done.33.a = bf16[256,512]{1,0:T(8,128)(2,1)S(1)} collective-permute-done((bf16[256,512]{1,0:T(8,128)(2,1)S(1)}, bf16[256,512]{1,0:T(8,128)(2,1)S(1)}, u32[]{:S(2)}, u32[]{:S(2)}) %collective-permute-start.33) | collective-permute-done | bytes 262176 | tf_op jit(solution)/shard_map/ppermute | solution.py:33
  154.5 3.2 collective-permute-start.36
  157.7 5.2 %collective-permute-done.35.refs_1_ = bf16[256,512]{1,0:T(8,128)(2,1)S(1)} collective-permute-done((bf16[256,512]{1,0:T(8,128)(2,1)S(1)}, bf16[256,512]{1,0:T(8,128)(2,1)S(1)}, u32[]{:S(2)}, u32[]{:S(2)}) %collective-permute-start.35) | collective-permute-done | bytes 262176 | tf_op jit(solution)/shard_map/ppermute | solution.py:33
  167.6 8.4 %mlp.6 = (bf16[4,256,512]{2,1,0:T(8,128)(2,1)S(1)}, bf16[4,256,512]{2,1,0:T(8,128)(2,1)S(1)}) custom-call(s32[4]{0:T(128)S(1)} %pad_add_fusion.flag.place, bf16[256,512]{1,0:T(8,128)(2,1)S(1)} %join.5.refs_0_.state, bf16[256,512]{1,0:T(8,128)(2,1)S(1)} %collective-permute-done.35.refs_1_, bf16[256,512]{1,0:T(8,128)(2,1)S(1)} %collective-permute-done.36.refs_2_, ...), custom_call_target="tpu_custom_call" | custom-call | tf_op jit(solution)/shard_map/mlp/pallas_call | solution.py:285
  179.2 3.1 collective-permute-start.44
  182.9 6.0 %collective-permute-done.43.a = bf16[256,512]{1,0:T(8,128)(2,1)S(1)} collective-permute-done((bf16[256,512]{1,0:T(8,128)(2,1)S(1)}, bf16[256,512]{1,0:T(8,128)(2,1)S(1)}, u32[]{:S(2)}, u32[]{:S(2)}) %collective-permute-start.43) | collective-permute-done | bytes 262176 | tf_op jit(solution)/shard_map/ppermute | solution.py:33
  188.9 4.6 %collective-permute-done.44.b = bf16[256,512]{1,0:T(8,128)(2,1)S(1)} collective-permute-done((bf16[256,512]{1,0:T(8,128)(2,1)S(1)}, bf16[256,512]{1,0:T(8,128)(2,1)S(1)}, u32[]{:S(2)}, u32[]{:S(2)}) %collective-permute-start.44) | collective-permute-done | bytes 262176 | tf_op jit(solution)/shard_map/ppermute | solution.py:33
  195.6 4.5 %collective-permute-start.46 = (bf16[256,512]{1,0:T(8,128)(2,1)S(1)}, bf16[256,512]{1,0:T(8,128)(2,1)S(1)}, u32[]{:S(2)}, u32[]{:S(2)}) collective-permute-start(bf16[256,512]{1,0:T(8,128)(2,1)S(1)} %total.6), channel_id=1, source_target_pairs={{0,16},{1,17},{2,18},{3,19},{4,20},{5,21},{6,22},{7,23},{8,24},{9,... | collective-permute-start | bytes 786440 | tf_op jit(solution)/shard_map/ppermute | solution.py:33
  200.1 6.0 %collective-permute-start.47 = (bf16[256,512]{1,0:T(8,128)(2,1)S(1)}, bf16[256,512]{1,0:T(8,128)(2,1)S(1)}, u32[]{:S(2)}, u32[]{:S(2)}) collective-permute-start(bf16[256,512]{1,0:T(8,128)(2,1)S(1)} %total.6), channel_id=1, source_target_pairs={{0,82},{1,83},{2,80},{3,81},{4,86},{5,87},{6,84},{7,85},{8,90},{9,... | collective-permute-start | bytes 786440 | tf_op jit(solution)/shard_map/ppermute | solution.py:33
  206.1 4.6 %collective-permute-done.46.a = bf16[256,512]{1,0:T(8,128)(2,1)S(1)} collective-permute-done((bf16[256,512]{1,0:T(8,128)(2,1)S(1)}, bf16[256,512]{1,0:T(8,128)(2,1)S(1)}, u32[]{:S(2)}, u32[]{:S(2)}) %collective-permute-start.46) | collective-permute-done | bytes 262176 | tf_op jit(solution)/shard_map/ppermute | solution.py:33
  215.2 6.7 %collective-permute-done.48.refs_1_ = bf16[256,512]{1,0:T(8,128)(2,1)S(1)} collective-permute-done((bf16[256,512]{1,0:T(8,128)(2,1)S(1)}, bf16[256,512]{1,0:T(8,128)(2,1)S(1)}, u32[]{:S(2)}, u32[]{:S(2)}) %collective-permute-start.48) | collective-permute-done | bytes 262176 | tf_op jit(solution)/shard_map/ppermute | solution.py:33
  226.9 8.6 %mlp.7 = (bf16[4,256,512]{2,1,0:T(8,128)(2,1)S(1)}, bf16[4,256,512]{2,1,0:T(8,128)(2,1)S(1)}, f32[8,640]{1,0:T(8,128)S(1)}, f32[8,512]{1,0:T(8,128)S(1)}) custom-call(s32[4]{0:T(128)S(1)} %pad_add_fusion.flag.place, bf16[256,512]{1,0:T(8,128)(2,1)S(1)} %join.6.refs_0_.state, bf16[256,512]{1,0:T(8,128)(2,1)S(1)} %collective-permute-done.48.refs_1_, ...), custom_call_target="tpu_custom_call" | custom-call | tf_op jit(solution)/shard_map/mlp/pallas_call | solution.py:285
  238.8 2.9 collective-permute-start.57
  242.4 5.8 %collective-permute-done.56.a = bf16[256,512]{1,0:T(8,128)(2,1)S(1)} collective-permute-done((bf16[256,512]{1,0:T(8,128)(2,1)S(1)}, bf16[256,512]{1,0:T(8,128)(2,1)S(1)}, u32[]{:S(2)}, u32[]{:S(2)}) %collective-permute-start.56) | collective-permute-done | bytes 262176 | tf_op jit(solution)/shard_map/ppermute | solution.py:33
  248.2 4.7 %collective-permute-done.57.b = bf16[256,512]{1,0:T(8,128)(2,1)S(1)} collective-permute-done((bf16[256,512]{1,0:T(8,128)(2,1)S(1)}, bf16[256,512]{1,0:T(8,128)(2,1)S(1)}, u32[]{:S(2)}, u32[]{:S(2)}) %collective-permute-start.57) | collective-permute-done | bytes 262176 | tf_op jit(solution)/shard_map/ppermute | solution.py:33
  255.0 3.1 collective-permute-start.59
  258.1 6.0 %collective-permute-start.60 = (bf16[256,512]{1,0:T(8,128)(2,1)S(1)}, bf16[256,512]{1,0:T(8,128)(2,1)S(1)}, u32[]{:S(2)}, u32[]{:S(2)}) collective-permute-start(bf16[256,512]{1,0:T(8,128)(2,1)S(1)} %total.7), channel_id=1, source_target_pairs={{0,82},{1,83},{2,80},{3,81},{4,86},{5,87},{6,84},{7,85},{8,90},{9,... | collective-permute-start | bytes 786440 | tf_op jit(solution)/shard_map/ppermute | solution.py:33
  264.1 4.7 %collective-permute-done.60.b = bf16[256,512]{1,0:T(8,128)(2,1)S(1)} collective-permute-done((bf16[256,512]{1,0:T(8,128)(2,1)S(1)}, bf16[256,512]{1,0:T(8,128)(2,1)S(1)}, u32[]{:S(2)}, u32[]{:S(2)}) %collective-permute-start.60) | collective-permute-done | bytes 262176 | tf_op jit(solution)/shard_map/ppermute | solution.py:33
  273.1 6.8 %collective-permute-done.61.refs_1_ = bf16[256,512]{1,0:T(8,128)(2,1)S(1)} collective-permute-done((bf16[256,512]{1,0:T(8,128)(2,1)S(1)}, bf16[256,512]{1,0:T(8,128)(2,1)S(1)}, u32[]{:S(2)}, u32[]{:S(2)}) %collective-permute-start.61) | collective-permute-done | bytes 262176 | tf_op jit(solution)/shard_map/ppermute | solution.py:33
  279.9 2.8 collective-permute-done.62.refs_2_
  292.3 10.4 %last_mlp.1 = (f32[16,16,256]{2,1,0:T(8,128)}, f32[8,512]{1,0:T(8,128)S(1)}) custom-call(s32[4]{0:T(128)S(1)} %pad_add_fusion.flag.place, bf16[256,512]{1,0:T(8,128)(2,1)S(1)} %join.7.refs_0_, bf16[256,512]{1,0:T(8,128)(2,1)S(1)} %collective-permute-done.61.refs_1_, bf16[256,512]{1,0:T(8,128)(2,1)S(1)} %collective-permute-done.62.refs_2_, ...), custom_call_target="tpu_custom_call" | custom-call | tf_op jit(solution)/shard_map/last_mlp/pallas_call | solution.py:285
  302.7 4.8 %all-to-all-start = ((f32[16,16,256]{2,1,0:T(8,128)}), f32[16,16,256]{2,1,0:T(8,128)S(1)}, u32[]{:S(2)}, u32[]{:S(2)}) async-start(f32[16,16,256]{2,1,0:T(8,128)} %get-tuple-element.68), calls=%async_computation | async-start | bytes 524288 | tf_op jit(solution)/shard_map/all_to_all | solution.py:426
  308.4 8.0 %all-to-all-done = f32[16,16,256]{2,1,0:T(8,128)S(1)} async-done(((f32[16,16,256]{2,1,0:T(8,128)}), f32[16,16,256]{2,1,0:T(8,128)S(1)}, u32[]{:S(2)}, u32[]{:S(2)}) %all-to-all-start) | async-done | bytes 262176 | tf_op jit(solution)/shard_map/all_to_all | solution.py:426
  317.2 4.8 %all-to-all-start.1 = ((bf16[32,16,256]{2,1,0:T(8,128)(2,1)}), bf16[32,16,256]{2,1,0:T(8,128)(2,1)S(1)}, u32[]{:S(2)}, u32[]{:S(2)}) async-start(bf16[32,16,256]{2,1,0:T(8,128)(2,1)} %broadcast_in_dim.6), calls=%async_computation.1 | async-start | bytes 524288 | tf_op jit(solution)/shard_map/all_to_all | solution.py:433
  322.9 8.1 %all-to-all-done.1 = bf16[32,16,256]{2,1,0:T(8,128)(2,1)S(1)} async-done(((bf16[32,16,256]{2,1,0:T(8,128)(2,1)}), bf16[32,16,256]{2,1,0:T(8,128)(2,1)S(1)}, u32[]{:S(2)}, u32[]{:S(2)}) %all-to-all-start.1) | async-done | bytes 262176 | tf_op jit(solution)/shard_map/all_to_all | solution.py:433
  331.7 3.3 head.1
  336.6 8.9 %all-to-all-start.2 = ((f32[128,8,128]{2,1,0:T(8,128)}), f32[128,8,128]{2,1,0:T(8,128)S(1)}, u32[]{:S(2)}, u32[]{:S(2)}) async-start(f32[128,8,128]{2,1,0:T(8,128)} %bitcast.11), calls=%async_computation.2 | async-start | bytes 1048576 | tf_op jit(solution)/shard_map/all_to_all | solution.py:453
  345.5 12.9 %all-to-all-done.2 = f32[128,8,128]{2,1,0:T(8,128)S(1)} async-done(((f32[128,8,128]{2,1,0:T(8,128)}), f32[128,8,128]{2,1,0:T(8,128)S(1)}, u32[]{:S(2)}, u32[]{:S(2)}) %all-to-all-start.2) | async-done | bytes 524320 | tf_op jit(solution)/shard_map/all_to_all | solution.py:453
  (158 shorter events, 89.7 us)
Async XLA Ops:
  18.1 10.1 %collective-permute-start.2 = (bf16[256,256]{1,0:T(8,128)(2,1)S(1)}, bf16[256,256]{1,0:T(8,128)(2,1)S(1)}, u32[]{:S(2)}, u32[]{:S(2)}) collective-permute-start(bf16[256,256]{1,0:T(8,128)(2,1)S(1)} %get-tuple-element.38.own.after), channel_id=1, source_target_pairs={{48,0},{49,1},{50,2},{51,3},{52,4},{53,5},{54,6},{55,7},{56,8},{57... | collective-permute-start | bytes 393224 | tf_op jit(solution)/shard_map/ppermute | solution.py:33
  19.4 8.8 %collective-permute-start.3 = (bf16[256,256]{1,0:T(8,128)(2,1)S(1)}, bf16[256,256]{1,0:T(8,128)(2,1)S(1)}, u32[]{:S(2)}, u32[]{:S(2)}) collective-permute-start(bf16[256,256]{1,0:T(8,128)(2,1)S(1)} %get-tuple-element.38.own.after), channel_id=1, source_target_pairs={{32,0},{33,1},{34,2},{35,3},{36,4},{37,5},{38,6},{39,7},{40,8},{41... | collective-permute-start | bytes 393224 | tf_op jit(solution)/shard_map/ppermute | solution.py:33
  35.1 8.6 %collective-permute-start.6 = (bf16[256,512]{1,0:T(8,128)(2,1)S(1)}, bf16[256,512]{1,0:T(8,128)(2,1)S(1)}, u32[]{:S(2)}, u32[]{:S(2)}) collective-permute-start(bf16[256,512]{1,0:T(8,128)(2,1)S(1)} %fresh.1.refs_0_.state), channel_id=1, source_target_pairs={{0,8},{1,9},{2,10},{3,11},{4,12},{5,13},{6,14},{7,15},{8,0},{9,1},... | collective-permute-start | bytes 786440 | tf_op jit(solution)/shard_map/ppermute | solution.py:33
  38.4 8.4 %collective-permute-start.7 = (bf16[256,512]{1,0:T(8,128)(2,1)S(1)}, bf16[256,512]{1,0:T(8,128)(2,1)S(1)}, u32[]{:S(2)}, u32[]{:S(2)}) collective-permute-start(bf16[256,512]{1,0:T(8,128)(2,1)S(1)} %fresh.1.refs_0_.state), channel_id=1, source_target_pairs={{0,12},{1,13},{2,14},{3,15},{4,0},{5,1},{6,2},{7,3},{8,4},{9,5},{1... | collective-permute-start | bytes 786440 | tf_op jit(solution)/shard_map/ppermute | solution.py:33
  40.4 12.6 %collective-permute-start.8 = (bf16[256,512]{1,0:T(8,128)(2,1)S(1)}, bf16[256,512]{1,0:T(8,128)(2,1)S(1)}, u32[]{:S(2)}, u32[]{:S(2)}) collective-permute-start(bf16[256,512]{1,0:T(8,128)(2,1)S(1)} %fresh.1.refs_0_.state), channel_id=1, source_target_pairs={{0,1},{1,0},{2,3},{3,2},{4,5},{5,4},{6,7},{7,6},{8,9},{9,8},{10,11... | collective-permute-start | bytes 786440 | tf_op jit(solution)/shard_map/ppermute | solution.py:33
  43.8 9.2 %collective-permute-start.10 = (bf16[256,512]{1,0:T(8,128)(2,1)S(1)}, bf16[256,512]{1,0:T(8,128)(2,1)S(1)}, u32[]{:S(2)}, u32[]{:S(2)}) collective-permute-start(bf16[256,512]{1,0:T(8,128)(2,1)S(1)} %collective-permute-done.6.refs_2_), channel_id=1, source_target_pairs={{0,1},{1,0},{2,3},{3,2},{4,5},{5,4},{6,7},{7,6},{8,9},{9,8},{10,11... | collective-permute-start | bytes 786440 | tf_op jit(solution)/shard_map/ppermute | solution.py:33
  64.4 10.0 %collective-permute-start.13 = (bf16[256,512]{1,0:T(8,128)(2,1)S(1)}, bf16[256,512]{1,0:T(8,128)(2,1)S(1)}, u32[]{:S(2)}, u32[]{:S(2)}) collective-permute-start(bf16[256,512]{1,0:T(8,128)(2,1)S(1)} %get-tuple-element.45), channel_id=1, source_target_pairs={{0,4},{1,5},{2,6},{3,7},{4,8},{5,9},{6,10},{7,11},{8,12},{9,13},{1... | collective-permute-start | bytes 786440 | tf_op jit(solution)/shard_map/ppermute | solution.py:33
  65.8 13.3 %collective-permute-start.14 = (bf16[256,512]{1,0:T(8,128)(2,1)S(1)}, bf16[256,512]{1,0:T(8,128)(2,1)S(1)}, u32[]{:S(2)}, u32[]{:S(2)}) collective-permute-start(bf16[256,512]{1,0:T(8,128)(2,1)S(1)} %get-tuple-element.46), channel_id=1, source_target_pairs={{0,12},{1,13},{2,14},{3,15},{4,0},{5,1},{6,2},{7,3},{8,4},{9,5},{1... | collective-permute-start | bytes 786440 | tf_op jit(solution)/shard_map/ppermute | solution.py:33
  67.7 12.8 %collective-permute-start.15 = (bf16[256,512]{1,0:T(8,128)(2,1)S(1)}, bf16[256,512]{1,0:T(8,128)(2,1)S(1)}, u32[]{:S(2)}, u32[]{:S(2)}) collective-permute-start(bf16[256,512]{1,0:T(8,128)(2,1)S(1)} %get-tuple-element.47), channel_id=1, source_target_pairs={{0,8},{1,9},{2,10},{3,11},{4,12},{5,13},{6,14},{7,15},{8,0},{9,1},... | collective-permute-start | bytes 786440 | tf_op jit(solution)/shard_map/ppermute | solution.py:33
  69.0 17.6 %collective-permute-start.18 = (bf16[256,256]{1,0:T(8,128)(2,1)S(1)}, bf16[256,256]{1,0:T(8,128)(2,1)S(1)}, u32[]{:S(2)}, u32[]{:S(2)}) collective-permute-start(bf16[256,256]{1,0:T(8,128)(2,1)S(1)} %get-tuple-element.48.own), channel_id=1, source_target_pairs={{16,0},{17,1},{18,2},{19,3},{20,4},{21,5},{22,6},{23,7},{24,8},{25... | collective-permute-start | bytes 393224 | tf_op jit(solution)/shard_map/ppermute | solution.py:33
  70.3 16.3 %collective-permute-start.19 = (bf16[256,256]{1,0:T(8,128)(2,1)S(1)}, bf16[256,256]{1,0:T(8,128)(2,1)S(1)}, u32[]{:S(2)}, u32[]{:S(2)}) collective-permute-start(bf16[256,256]{1,0:T(8,128)(2,1)S(1)} %get-tuple-element.48.own), channel_id=1, source_target_pairs={{48,0},{49,1},{50,2},{51,3},{52,4},{53,5},{54,6},{55,7},{56,8},{57... | collective-permute-start | bytes 393224 | tf_op jit(solution)/shard_map/ppermute | solution.py:33
  74.5 12.1 %collective-permute-start.20 = (bf16[256,256]{1,0:T(8,128)(2,1)S(1)}, bf16[256,256]{1,0:T(8,128)(2,1)S(1)}, u32[]{:S(2)}, u32[]{:S(2)}) collective-permute-start(bf16[256,256]{1,0:T(8,128)(2,1)S(1)} %get-tuple-element.48.own), channel_id=1, source_target_pairs={{32,0},{33,1},{34,2},{35,3},{36,4},{37,5},{38,6},{39,7},{40,8},{41... | collective-permute-start | bytes 393224 | tf_op jit(solution)/shard_map/ppermute | solution.py:33
  81.2 14.3 %collective-permute-start.16 = (bf16[256,512]{1,0:T(8,128)(2,1)S(1)}, bf16[256,512]{1,0:T(8,128)(2,1)S(1)}, u32[]{:S(2)}, u32[]{:S(2)}) collective-permute-start(bf16[256,512]{1,0:T(8,128)(2,1)S(1)} %total.4), channel_id=1, source_target_pairs={{0,16},{1,17},{2,18},{3,19},{4,20},{5,21},{6,22},{7,23},{8,24},{9,... | collective-permute-start | bytes 786440 | tf_op jit(solution)/shard_map/ppermute | solution.py:33
  82.5 13.0 %collective-permute-start.17 = (bf16[256,512]{1,0:T(8,128)(2,1)S(1)}, bf16[256,512]{1,0:T(8,128)(2,1)S(1)}, u32[]{:S(2)}, u32[]{:S(2)}) collective-permute-start(bf16[256,512]{1,0:T(8,128)(2,1)S(1)} %total.4), channel_id=1, source_target_pairs={{0,82},{1,83},{2,80},{3,81},{4,86},{5,87},{6,84},{7,85},{8,90},{9,... | collective-permute-start | bytes 786440 | tf_op jit(solution)/shard_map/ppermute | solution.py:33
  86.7 8.8 %collective-permute-start.21 = (bf16[256,256]{1,0:T(8,128)(2,1)S(1)}, bf16[256,256]{1,0:T(8,128)(2,1)S(1)}, u32[]{:S(2)}, u32[]{:S(2)}) collective-permute-start(bf16[256,256]{1,0:T(8,128)(2,1)S(1)} %gathered.3.own), channel_id=1, source_target_pairs={{0,66},{1,67},{2,64},{3,65},{4,70},{5,71},{6,68},{7,69},{8,74},{9,... | collective-permute-start | bytes 393224 | tf_op jit(solution)/shard_map/ppermute | solution.py:33
  96.2 13.0 %collective-permute-start.22 = (bf16[256,512]{1,0:T(8,128)(2,1)S(1)}, bf16[256,512]{1,0:T(8,128)(2,1)S(1)}, u32[]{:S(2)}, u32[]{:S(2)}) collective-permute-start(bf16[256,512]{1,0:T(8,128)(2,1)S(1)} %join.4.refs_0_.state), channel_id=1, source_target_pairs={{0,4},{1,5},{2,6},{3,7},{4,8},{5,9},{6,10},{7,11},{8,12},{9,13},{1... | collective-permute-start | bytes 786440 | tf_op jit(solution)/shard_map/ppermute | solution.py:33
  97.1 12.0 %collective-permute-start.23 = (bf16[256,512]{1,0:T(8,128)(2,1)S(1)}, bf16[256,512]{1,0:T(8,128)(2,1)S(1)}, u32[]{:S(2)}, u32[]{:S(2)}) collective-permute-start(bf16[256,512]{1,0:T(8,128)(2,1)S(1)} %join.4.refs_0_.state), channel_id=1, source_target_pairs={{0,8},{1,9},{2,10},{3,11},{4,12},{5,13},{6,14},{7,15},{8,0},{9,1},... | collective-permute-start | bytes 786440 | tf_op jit(solution)/shard_map/ppermute | solution.py:33
  99.1 10.6 %collective-permute-start.24 = (bf16[256,512]{1,0:T(8,128)(2,1)S(1)}, bf16[256,512]{1,0:T(8,128)(2,1)S(1)}, u32[]{:S(2)}, u32[]{:S(2)}) collective-permute-start(bf16[256,512]{1,0:T(8,128)(2,1)S(1)} %join.4.refs_0_.state), channel_id=1, source_target_pairs={{0,12},{1,13},{2,14},{3,15},{4,0},{5,1},{6,2},{7,3},{8,4},{9,5},{1... | collective-permute-start | bytes 786440 | tf_op jit(solution)/shard_map/ppermute | solution.py:33
  99.8 10.1 %collective-permute-start.25 = (bf16[256,512]{1,0:T(8,128)(2,1)S(1)}, bf16[256,512]{1,0:T(8,128)(2,1)S(1)}, u32[]{:S(2)}, u32[]{:S(2)}) collective-permute-start(bf16[256,512]{1,0:T(8,128)(2,1)S(1)} %join.4.refs_0_.state), channel_id=1, source_target_pairs={{0,1},{1,0},{2,3},{3,2},{4,5},{5,4},{6,7},{7,6},{8,9},{9,8},{10,11... | collective-permute-start | bytes 786440 | tf_op jit(solution)/shard_map/ppermute | solution.py:33
  122.8 9.9 %collective-permute-start.30 = (bf16[256,512]{1,0:T(8,128)(2,1)S(1)}, bf16[256,512]{1,0:T(8,128)(2,1)S(1)}, u32[]{:S(2)}, u32[]{:S(2)}) collective-permute-start(bf16[256,512]{1,0:T(8,128)(2,1)S(1)} %get-tuple-element.52), channel_id=1, source_target_pairs={{0,4},{1,5},{2,6},{3,7},{4,8},{5,9},{6,10},{7,11},{8,12},{9,13},{1... | collective-permute-start | bytes 786440 | tf_op jit(solution)/shard_map/ppermute | solution.py:33
  123.1 14.2 %collective-permute-start.31 = (bf16[256,512]{1,0:T(8,128)(2,1)S(1)}, bf16[256,512]{1,0:T(8,128)(2,1)S(1)}, u32[]{:S(2)}, u32[]{:S(2)}) collective-permute-start(bf16[256,512]{1,0:T(8,128)(2,1)S(1)} %get-tuple-element.53), channel_id=1, source_target_pairs={{0,12},{1,13},{2,14},{3,15},{4,0},{5,1},{6,2},{7,3},{8,4},{9,5},{1... | collective-permute-start | bytes 786440 | tf_op jit(solution)/shard_map/ppermute | solution.py:33
  126.1 12.5 %collective-permute-start.32 = (bf16[256,512]{1,0:T(8,128)(2,1)S(1)}, bf16[256,512]{1,0:T(8,128)(2,1)S(1)}, u32[]{:S(2)}, u32[]{:S(2)}) collective-permute-start(bf16[256,512]{1,0:T(8,128)(2,1)S(1)} %get-tuple-element.54), channel_id=1, source_target_pairs={{0,8},{1,9},{2,10},{3,11},{4,12},{5,13},{6,14},{7,15},{8,0},{9,1},... | collective-permute-start | bytes 786440 | tf_op jit(solution)/shard_map/ppermute | solution.py:33
  139.3 13.6 %collective-permute-start.33 = (bf16[256,512]{1,0:T(8,128)(2,1)S(1)}, bf16[256,512]{1,0:T(8,128)(2,1)S(1)}, u32[]{:S(2)}, u32[]{:S(2)}) collective-permute-start(bf16[256,512]{1,0:T(8,128)(2,1)S(1)} %total.5), channel_id=1, source_target_pairs={{0,16},{1,17},{2,18},{3,19},{4,20},{5,21},{6,22},{7,23},{8,24},{9,... | collective-permute-start | bytes 786440 | tf_op jit(solution)/shard_map/ppermute | solution.py:33
  142.4 10.6 %collective-permute-start.34 = (bf16[256,512]{1,0:T(8,128)(2,1)S(1)}, bf16[256,512]{1,0:T(8,128)(2,1)S(1)}, u32[]{:S(2)}, u32[]{:S(2)}) collective-permute-start(bf16[256,512]{1,0:T(8,128)(2,1)S(1)} %total.5), channel_id=1, source_target_pairs={{0,82},{1,83},{2,80},{3,81},{4,86},{5,87},{6,84},{7,85},{8,90},{9,... | collective-permute-start | bytes 786440 | tf_op jit(solution)/shard_map/ppermute | solution.py:33
  153.6 9.4 %collective-permute-start.35 = (bf16[256,512]{1,0:T(8,128)(2,1)S(1)}, bf16[256,512]{1,0:T(8,128)(2,1)S(1)}, u32[]{:S(2)}, u32[]{:S(2)}) collective-permute-start(bf16[256,512]{1,0:T(8,128)(2,1)S(1)} %join.5.refs_0_.state), channel_id=1, source_target_pairs={{0,4},{1,5},{2,6},{3,7},{4,8},{5,9},{6,10},{7,11},{8,12},{9,13},{1... | collective-permute-start | bytes 786440 | tf_op jit(solution)/shard_map/ppermute | solution.py:33
  154.5 11.2 %collective-permute-start.36 = (bf16[256,512]{1,0:T(8,128)(2,1)S(1)}, bf16[256,512]{1,0:T(8,128)(2,1)S(1)}, u32[]{:S(2)}, u32[]{:S(2)}) collective-permute-start(bf16[256,512]{1,0:T(8,128)(2,1)S(1)} %join.5.refs_0_.state), channel_id=1, source_target_pairs={{0,8},{1,9},{2,10},{3,11},{4,12},{5,13},{6,14},{7,15},{8,0},{9,1},... | collective-permute-start | bytes 786440 | tf_op jit(solution)/shard_map/ppermute | solution.py:33
  157.7 8.6 %collective-permute-start.38 = (bf16[256,512]{1,0:T(8,128)(2,1)S(1)}, bf16[256,512]{1,0:T(8,128)(2,1)S(1)}, u32[]{:S(2)}, u32[]{:S(2)}) collective-permute-start(bf16[256,512]{1,0:T(8,128)(2,1)S(1)} %join.5.refs_0_.state), channel_id=1, source_target_pairs={{0,1},{1,0},{2,3},{3,2},{4,5},{5,4},{6,7},{7,6},{8,9},{9,8},{10,11... | collective-permute-start | bytes 786440 | tf_op jit(solution)/shard_map/ppermute | solution.py:33
  179.0 9.9 %collective-permute-start.43 = (bf16[256,512]{1,0:T(8,128)(2,1)S(1)}, bf16[256,512]{1,0:T(8,128)(2,1)S(1)}, u32[]{:S(2)}, u32[]{:S(2)}) collective-permute-start(bf16[256,512]{1,0:T(8,128)(2,1)S(1)} %get-tuple-element.58), channel_id=1, source_target_pairs={{0,4},{1,5},{2,6},{3,7},{4,8},{5,9},{6,10},{7,11},{8,12},{9,13},{1... | collective-permute-start | bytes 786440 | tf_op jit(solution)/shard_map/ppermute | solution.py:33
  179.2 14.3 %collective-permute-start.44 = (bf16[256,512]{1,0:T(8,128)(2,1)S(1)}, bf16[256,512]{1,0:T(8,128)(2,1)S(1)}, u32[]{:S(2)}, u32[]{:S(2)}) collective-permute-start(bf16[256,512]{1,0:T(8,128)(2,1)S(1)} %get-tuple-element.59), channel_id=1, source_target_pairs={{0,12},{1,13},{2,14},{3,15},{4,0},{5,1},{6,2},{7,3},{8,4},{9,5},{1... | collective-permute-start | bytes 786440 | tf_op jit(solution)/shard_map/ppermute | solution.py:33
  182.3 12.5 %collective-permute-start.45 = (bf16[256,512]{1,0:T(8,128)(2,1)S(1)}, bf16[256,512]{1,0:T(8,128)(2,1)S(1)}, u32[]{:S(2)}, u32[]{:S(2)}) collective-permute-start(bf16[256,512]{1,0:T(8,128)(2,1)S(1)} %get-tuple-element.60), channel_id=1, source_target_pairs={{0,8},{1,9},{2,10},{3,11},{4,12},{5,13},{6,14},{7,15},{8,0},{9,1},... | collective-permute-start | bytes 786440 | tf_op jit(solution)/shard_map/ppermute | solution.py:33
  195.6 15.1 %collective-permute-start.46 = (bf16[256,512]{1,0:T(8,128)(2,1)S(1)}, bf16[256,512]{1,0:T(8,128)(2,1)S(1)}, u32[]{:S(2)}, u32[]{:S(2)}) collective-permute-start(bf16[256,512]{1,0:T(8,128)(2,1)S(1)} %total.6), channel_id=1, source_target_pairs={{0,16},{1,17},{2,18},{3,19},{4,20},{5,21},{6,22},{7,23},{8,24},{9,... | collective-permute-start | bytes 786440 | tf_op jit(solution)/shard_map/ppermute | solution.py:33
  200.1 10.7 %collective-permute-start.47 = (bf16[256,512]{1,0:T(8,128)(2,1)S(1)}, bf16[256,512]{1,0:T(8,128)(2,1)S(1)}, u32[]{:S(2)}, u32[]{:S(2)}) collective-permute-start(bf16[256,512]{1,0:T(8,128)(2,1)S(1)} %total.6), channel_id=1, source_target_pairs={{0,82},{1,83},{2,80},{3,81},{4,86},{5,87},{6,84},{7,85},{8,90},{9,... | collective-permute-start | bytes 786440 | tf_op jit(solution)/shard_map/ppermute | solution.py:33
  211.4 10.5 %collective-permute-start.48 = (bf16[256,512]{1,0:T(8,128)(2,1)S(1)}, bf16[256,512]{1,0:T(8,128)(2,1)S(1)}, u32[]{:S(2)}, u32[]{:S(2)}) collective-permute-start(bf16[256,512]{1,0:T(8,128)(2,1)S(1)} %join.6.refs_0_.state), channel_id=1, source_target_pairs={{0,4},{1,5},{2,6},{3,7},{4,8},{5,9},{6,10},{7,11},{8,12},{9,13},{1... | collective-permute-start | bytes 786440 | tf_op jit(solution)/shard_map/ppermute | solution.py:33
  212.4 12.4 %collective-permute-start.49 = (bf16[256,512]{1,0:T(8,128)(2,1)S(1)}, bf16[256,512]{1,0:T(8,128)(2,1)S(1)}, u32[]{:S(2)}, u32[]{:S(2)}) collective-permute-start(bf16[256,512]{1,0:T(8,128)(2,1)S(1)} %join.6.refs_0_.state), channel_id=1, source_target_pairs={{0,8},{1,9},{2,10},{3,11},{4,12},{5,13},{6,14},{7,15},{8,0},{9,1},... | collective-permute-start | bytes 786440 | tf_op jit(solution)/shard_map/ppermute | solution.py:33
  215.1 10.3 %collective-permute-start.50 = (bf16[256,512]{1,0:T(8,128)(2,1)S(1)}, bf16[256,512]{1,0:T(8,128)(2,1)S(1)}, u32[]{:S(2)}, u32[]{:S(2)}) collective-permute-start(bf16[256,512]{1,0:T(8,128)(2,1)S(1)} %join.6.refs_0_.state), channel_id=1, source_target_pairs={{0,12},{1,13},{2,14},{3,15},{4,0},{5,1},{6,2},{7,3},{8,4},{9,5},{1... | collective-permute-start | bytes 786440 | tf_op jit(solution)/shard_map/ppermute | solution.py:33
  215.2 10.1 %collective-permute-start.51 = (bf16[256,512]{1,0:T(8,128)(2,1)S(1)}, bf16[256,512]{1,0:T(8,128)(2,1)S(1)}, u32[]{:S(2)}, u32[]{:S(2)}) collective-permute-start(bf16[256,512]{1,0:T(8,128)(2,1)S(1)} %join.6.refs_0_.state), channel_id=1, source_target_pairs={{0,1},{1,0},{2,3},{3,2},{4,5},{5,4},{6,7},{7,6},{8,9},{9,8},{10,11... | collective-permute-start | bytes 786440 | tf_op jit(solution)/shard_map/ppermute | solution.py:33
  238.4 9.8 %collective-permute-start.56 = (bf16[256,512]{1,0:T(8,128)(2,1)S(1)}, bf16[256,512]{1,0:T(8,128)(2,1)S(1)}, u32[]{:S(2)}, u32[]{:S(2)}) collective-permute-start(bf16[256,512]{1,0:T(8,128)(2,1)S(1)} %get-tuple-element.64), channel_id=1, source_target_pairs={{0,4},{1,5},{2,6},{3,7},{4,8},{5,9},{6,10},{7,11},{8,12},{9,13},{1... | collective-permute-start | bytes 786440 | tf_op jit(solution)/shard_map/ppermute | solution.py:33
  238.8 14.1 %collective-permute-start.57 = (bf16[256,512]{1,0:T(8,128)(2,1)S(1)}, bf16[256,512]{1,0:T(8,128)(2,1)S(1)}, u32[]{:S(2)}, u32[]{:S(2)}) collective-permute-start(bf16[256,512]{1,0:T(8,128)(2,1)S(1)} %get-tuple-element.65), channel_id=1, source_target_pairs={{0,12},{1,13},{2,14},{3,15},{4,0},{5,1},{6,2},{7,3},{8,4},{9,5},{1... | collective-permute-start | bytes 786440 | tf_op jit(solution)/shard_map/ppermute | solution.py:33
  241.7 12.6 %collective-permute-start.58 = (bf16[256,512]{1,0:T(8,128)(2,1)S(1)}, bf16[256,512]{1,0:T(8,128)(2,1)S(1)}, u32[]{:S(2)}, u32[]{:S(2)}) collective-permute-start(bf16[256,512]{1,0:T(8,128)(2,1)S(1)} %get-tuple-element.66), channel_id=1, source_target_pairs={{0,8},{1,9},{2,10},{3,11},{4,12},{5,13},{6,14},{7,15},{8,0},{9,1},... | collective-permute-start | bytes 786440 | tf_op jit(solution)/shard_map/ppermute | solution.py:33
  255.0 9.1 %collective-permute-start.59 = (bf16[256,512]{1,0:T(8,128)(2,1)S(1)}, bf16[256,512]{1,0:T(8,128)(2,1)S(1)}, u32[]{:S(2)}, u32[]{:S(2)}) collective-permute-start(bf16[256,512]{1,0:T(8,128)(2,1)S(1)} %total.7), channel_id=1, source_target_pairs={{0,16},{1,17},{2,18},{3,19},{4,20},{5,21},{6,22},{7,23},{8,24},{9,... | collective-permute-start | bytes 786440 | tf_op jit(solution)/shard_map/ppermute | solution.py:33
  258.1 10.7 %collective-permute-start.60 = (bf16[256,512]{1,0:T(8,128)(2,1)S(1)}, bf16[256,512]{1,0:T(8,128)(2,1)S(1)}, u32[]{:S(2)}, u32[]{:S(2)}) collective-permute-start(bf16[256,512]{1,0:T(8,128)(2,1)S(1)} %total.7), channel_id=1, source_target_pairs={{0,82},{1,83},{2,80},{3,81},{4,86},{5,87},{6,84},{7,85},{8,90},{9,... | collective-permute-start | bytes 786440 | tf_op jit(solution)/shard_map/ppermute | solution.py:33
  269.4 10.5 %collective-permute-start.61 = (bf16[256,512]{1,0:T(8,128)(2,1)S(1)}, bf16[256,512]{1,0:T(8,128)(2,1)S(1)}, u32[]{:S(2)}, u32[]{:S(2)}) collective-permute-start(bf16[256,512]{1,0:T(8,128)(2,1)S(1)} %join.7.refs_0_), channel_id=1, source_target_pairs={{0,4},{1,5},{2,6},{3,7},{4,8},{5,9},{6,10},{7,11},{8,12},{9,13},{1... | collective-permute-start | bytes 786440 | tf_op jit(solution)/shard_map/ppermute | solution.py:33
  270.3 12.4 %collective-permute-start.62 = (bf16[256,512]{1,0:T(8,128)(2,1)S(1)}, bf16[256,512]{1,0:T(8,128)(2,1)S(1)}, u32[]{:S(2)}, u32[]{:S(2)}) collective-permute-start(bf16[256,512]{1,0:T(8,128)(2,1)S(1)} %join.7.refs_0_), channel_id=1, source_target_pairs={{0,8},{1,9},{2,10},{3,11},{4,12},{5,13},{6,14},{7,15},{8,0},{9,1},... | collective-permute-start | bytes 786440 | tf_op jit(solution)/shard_map/ppermute | solution.py:33
  273.0 10.3 %collective-permute-start.63 = (bf16[256,512]{1,0:T(8,128)(2,1)S(1)}, bf16[256,512]{1,0:T(8,128)(2,1)S(1)}, u32[]{:S(2)}, u32[]{:S(2)}) collective-permute-start(bf16[256,512]{1,0:T(8,128)(2,1)S(1)} %join.7.refs_0_), channel_id=1, source_target_pairs={{0,12},{1,13},{2,14},{3,15},{4,0},{5,1},{6,2},{7,3},{8,4},{9,5},{1... | collective-permute-start | bytes 786440 | tf_op jit(solution)/shard_map/ppermute | solution.py:33
  273.1 10.2 %collective-permute-start.64 = (bf16[256,512]{1,0:T(8,128)(2,1)S(1)}, bf16[256,512]{1,0:T(8,128)(2,1)S(1)}, u32[]{:S(2)}, u32[]{:S(2)}) collective-permute-start(bf16[256,512]{1,0:T(8,128)(2,1)S(1)} %join.7.refs_0_), channel_id=1, source_target_pairs={{0,1},{1,0},{2,3},{3,2},{4,5},{5,4},{6,7},{7,6},{8,9},{9,8},{10,11... | collective-permute-start | bytes 786440 | tf_op jit(solution)/shard_map/ppermute | solution.py:33
  302.7 13.7 %all-to-all-start = ((f32[16,16,256]{2,1,0:T(8,128)}), f32[16,16,256]{2,1,0:T(8,128)S(1)}, u32[]{:S(2)}, u32[]{:S(2)}) async-start(f32[16,16,256]{2,1,0:T(8,128)} %get-tuple-element.68), calls=%async_computation | async-start | bytes 524288 | tf_op jit(solution)/shard_map/all_to_all | solution.py:426
  317.2 13.8 %all-to-all-start.1 = ((bf16[32,16,256]{2,1,0:T(8,128)(2,1)}), bf16[32,16,256]{2,1,0:T(8,128)(2,1)S(1)}, u32[]{:S(2)}, u32[]{:S(2)}) async-start(bf16[32,16,256]{2,1,0:T(8,128)(2,1)} %broadcast_in_dim.6), calls=%async_computation.1 | async-start | bytes 524288 | tf_op jit(solution)/shard_map/all_to_all | solution.py:433
  336.6 21.8 %all-to-all-start.2 = ((f32[128,8,128]{2,1,0:T(8,128)}), f32[128,8,128]{2,1,0:T(8,128)S(1)}, u32[]{:S(2)}, u32[]{:S(2)}) async-start(f32[128,8,128]{2,1,0:T(8,128)} %bitcast.11), calls=%async_computation.2 | async-start | bytes 1048576 | tf_op jit(solution)/shard_map/all_to_all | solution.py:453
  (33 other events, 673.3 us)
where the time goes:
time: 361 us; the launch traced here: 359 us
  waiting for transfers between devices  170 us (47%)
  starting transfers between devices  102 us (28%)
  Pallas kernels  72 us (20%)
  local copies, waits for them, and re-layouts  12.3 us (3%)
    ppermute x68, waiting for transfers between devices, moved(): return lax.ppermute(value, AXES, pairs)  141 us
    ppermute x68, starting transfers between devices, moved(): return lax.ppermute(value, AXES, pairs)  83.7 us
    pallas_call x20, Pallas kernels, local(): pl.pallas_call(kernel, in_specs=[SMEM_SPEC] * len(scalars) + [VMEM_SPEC]...  51.2 us
    all_to_all x1, waiting for transfers between devices, per_device(): lax.all_to_all(parts, AXES, 0, 0, tiled=True).reshape(2, 4, 16, 8, 128)  12.9 us
    pallas_call x1, Pallas kernels, embed_parts(): pl.pallas_call(functools.partial(embed_kernel, width), in_specs=[VMEM_SPE...  11.9 us
    all_to_all x1, starting transfers between devices, per_device(): lax.all_to_all(parts, AXES, 0, 0, tiled=True).reshape(2, 4, 16, 8, 128)  8.87 us
    unnamed x21, local copies, waits for them, and re-layouts  8.18 us
    all_to_all x1, waiting for transfers between devices, per_device(): lax.all_to_all(jnp.broadcast_to(value, (32, *value.shape)), ('dp', 'mp'),...  8.1 us
  transfers between devices with their start and end apart: 71, of which 51 were waited for; matrix products, arithmetic and copies ran while one was open for 0% of the time, Pallas kernels for 2%

commit v1 on v0

--- a/solution.py
+++ b/solution.py
@@ -7,8 +7,10 @@
 from jax.experimental.pallas import tpu as pltpu
 from jax.sharding import PartitionSpec as P
 
+
 GROUP = 8
 BLOCKS = 2
+STREAMS = 1
 AXES = ("dp", "section", "mp")
 
 norm_eps = 1e-05
@@ -49,21 +51,21 @@
     return moved(value, lambda d, z, x, y, c: (1 - d, z, x, 1 - y, c))
 
 
-def to_first(value, source):
-    return moved(value, lambda d, z, x, y, c: (d, 0, x, y, c) if z == source else None)
+def along_sections(value, shift):
+    return moved(value, lambda d, z, x, y, c: (d, (z + shift) % 4, x, y, c))
 
 
 def onward(value, flip):
-    return moved(value, lambda d, z, x, y, c: (d ^ flip, z + 1, x, y ^ flip, c) if z < 3 else None)
+    return moved(value, lambda d, z, x, y, c: (d ^ flip, (z + 1) % 4, x, y ^ flip, c))
 
 
 def nt_dot(a, b):
     return lax.dot_general(a, b, (((1,), (1,)), ((), ())), preferred_element_type=f32)
 
 
-def embed_kernel(width, ids_ref, table_ref, *refs):
-    outs, (held, sems) = refs[:-2], refs[-2:]
-    rows = ids_ref.shape[0]
+def embed_kernel(width, first, place, ids_ref, table_ref, out, held, sems):
+    rows = out.shape[0]
+    ids = ids_ref[first : first + rows, :]
     steps = table_ref.shape[1] // width
 
     def copy(step):
@@ -79,13 +81,15 @@
     def one(step, acc):
         copy(step).wait()
         start = pl.multiple_of(step * width, width)
-        hot = lax.broadcasted_iota(jnp.int32, (rows, width), 1) == ids_ref[...] - start
+        hot = lax.broadcasted_iota(jnp.int32, (rows, width), 1) == ids - start
         return acc + nt_dot(hot.astype(f32).astype(bf16), held[:, pl.ds(start, width)])
 
     acc = lax.fori_loop(0, steps, one, jnp.zeros((rows, table_ref.shape[0]), f32))
-    count = rows // len(outs)
-    for i, out in enumerate(outs):
-        out[...] = acc[i * count : (i + 1) * count].astype(bf16)
+    out[...] = acc.astype(bf16)
+
+
+def cost(products):
+    return pl.CostEstimate(flops=2 * products, bytes_accessed=0, transcendentals=0)
 
 
 def in_hbm(value):
@@ -101,21 +105,21 @@
 SMEM_SPEC = pl.BlockSpec(memory_space=pltpu.SMEM)
 
 
-def embed_parts(ids, table, count):
+def embed_part(place, ids, first, rows, table):
     width = 1024
-    rows = ids.shape[0] // count
     return pl.pallas_call(
-        functools.partial(embed_kernel, width),
-        in_specs=[VMEM_SPEC, HBM_SPEC],
-        out_specs=[VMEM_SPEC] * count,
-        out_shape=[pltpu.VMEM((rows, table.shape[0]), bf16)] * count,
+        functools.partial(embed_kernel, width, first),
+        in_specs=[SMEM_SPEC, VMEM_SPEC, HBM_SPEC],
+        out_specs=VMEM_SPEC,
+        out_shape=pltpu.VMEM((rows, table.shape[0]), bf16),
         scratch_shapes=[
             pltpu.VMEM(table.shape, bf16),
             pltpu.SemaphoreType.DMA((table.shape[1] // width,)),
         ],
-        compiler_params=pltpu.CompilerParams(vmem_limit_bytes=24 * 1024 * 1024),
+        compiler_params=pltpu.CompilerParams(vmem_limit_bytes=14 * 1024 * 1024),
+        cost_estimate=cost(rows * table.size),
         name="embed",
-    )(in_vmem(ids), in_hbm(table))
+    )(place, in_vmem(ids), in_hbm(table))
 
 
 def load_kernel(count, after, *refs):
@@ -169,8 +173,11 @@
     lax.fori_loop(0, chunks[0].shape[0] // 32, one, 0)
 
 
-def hidden_units(scaled, wg, wu, inverse_ref, gate_ref, up_ref):
+def hidden_units(scaled, wg, wu, inverse_ref, gate_ref, up_ref, wait=None):
     def one(k, carry):
+        if wait is not None:
+            wait(0, k)
+            wait(1, k)
         cols = pl.ds(pl.multiple_of(k * 1024, 1024), 1024)
         part = scaled[:, cols]
         gate = jnp.dot(part, wg[0, cols, :], preferred_element_type=f32)
@@ -218,13 +225,32 @@
 
 
 def last_kernel(count, place, *refs):
-    chunks, (gain, wg, wu, wd) = refs[:8], refs[8:12]
-    before = refs[12 : 12 + count]
+    chunks, gain, before, far = refs[:8], refs[8], refs[9 : 9 + count], refs[9 + count : 12 + count]
     out, base = refs[12 + count : 14 + count]
+    held, sems = refs[-8:-5], refs[-5]
     scaled, inverse, gate, up = refs[-4:]
-    x, c = place[0], place[1]
-    prepare(x, c, chunks, gain, scaled, inverse)
-    hidden = hidden_units(scaled, wg, wu, inverse, gate, up)
+
+    def copy(kind, k):
+        rows = pl.ds(pl.multiple_of(k * 1024, 1024), 1024)
+        return pltpu.make_async_copy(
+            far[kind].at[0, rows, :], held[kind].at[0, rows, :], sems.at[kind * 4 + k]
+        )
+
+    def begin(k, carry):
+        copy(0, k).start()
+        copy(1, k).start()
+        return carry
+
+    def begin_down(k, carry):
+        copy(2, k).start()
+        return carry
+
+    lax.fori_loop(0, 4, begin, 0)
+    lax.fori_loop(0, 4, begin_down, 0)
+    prepare(place[0], place[1], chunks, gain, scaled, inverse)
+    hidden = hidden_units(
+        scaled, held[0], held[1], inverse, gate, up, lambda kind, k: copy(kind, k).wait()
+    )
     base[...] = mean_tokens(chunks[0][...].astype(f32))
     every = jnp.concatenate([ref[...] for ref in before] + [mean_tokens(hidden)], axis=0)
     high = every.astype(bf16)
@@ -232,12 +258,15 @@
     rows = every.shape[0]
     stacked = jnp.concatenate([high, low], axis=0)
 
-    def one(m, carry):
-        term = nt_dot(stacked, wd[0, pl.ds(pl.multiple_of(m * 256, 256), 256), :])
-        out[m] = term[:rows] + term[rows:]
-        return carry
-
-    lax.fori_loop(0, 16, one, 0)
+    def one(k, carry):
+        copy(2, k).wait()
+        term = nt_dot(stacked, held[2][0, pl.ds(pl.multiple_of(k * 1024, 1024), 1024), :])
+        term = term[:rows] + term[rows:]
+        for m in range(4):
+            out[4 * k + m] = term[:, m * 256 : (m + 1) * 256]
+        return carry
+
+    lax.fori_loop(0, 4, one, 0)
 
 
 def gathered_kernel(own, a, b, d, out):
@@ -254,8 +283,11 @@
     )
 
 
-def fresh_kernel(flag, own, peer, out):
-    out[...] = by_y(flag, own, peer).astype(bf16)
+def fresh_kernel(flag, own, peer, *out):
+    whole = by_y(flag, own, peer).astype(bf16)
+    rows = out[0].shape[0]
+    for i, ref in enumerate(out):
+        ref[...] = whole[i * rows : (i + 1) * rows]
 
 
 def halves_kernel(keep, got, own, *out):
@@ -275,22 +307,21 @@
     out[...] = (a[...].astype(f32) + b[...].astype(f32)).astype(bf16)
 
 
-def join_fresh_kernel(flag, a, b, own, peer, out):
-    joined = a[...].astype(f32) + b[...].astype(f32)
-    out[...] = jnp.where(flag[3] == 0, by_y(flag, own, peer), joined).astype(bf16)
-
-
-def local(kernel, scalars, values, outs, scratch=(), name=None):
+def join_fresh_kernel(flag, a, b, fresh, out):
+    joined = (a[...].astype(f32) + b[...].astype(f32)).astype(bf16)
+    out[...] = jnp.where(flag[3] == 0, fresh[...], joined)
+
+
+def local(kernel, scalars, values, outs, scratch=(), limit=4, far=()):
     single = not isinstance(outs, list)
     return pl.pallas_call(
         kernel,
-        in_specs=[SMEM_SPEC] * len(scalars) + [VMEM_SPEC] * len(values),
+        in_specs=[SMEM_SPEC] * len(scalars) + [VMEM_SPEC] * len(values) + [HBM_SPEC] * len(far),
         out_specs=VMEM_SPEC if single else [VMEM_SPEC] * len(outs),
         out_shape=outs,
         scratch_shapes=list(scratch),
-        compiler_params=pltpu.CompilerParams(vmem_limit_bytes=20 * 1024 * 1024),
-        name=name,
-    )(*scalars, *[in_vmem(v) for v in values])
+        compiler_params=pltpu.CompilerParams(vmem_limit_bytes=limit * 1024 * 1024),
+    )(*scalars, *[in_vmem(v) for v in values], *[in_hbm(v) for v in far])
 
 
 def out_vmem(shape, dtype):
@@ -313,18 +344,20 @@
         outs += [out_vmem((tokens // 32, 640), f32), out_vmem((tokens // 32, 512), f32)]
     return local(
         functools.partial(mlp_kernel, pool), [place], [*mine, *theirs, gain, *weights], outs,
-        mlp_scratch(tokens), "mlp",
-    )
-
-
-def call_last(place, mine, theirs, gain, weights, before):
+        mlp_scratch(tokens), 16,
+    )
+
+
+def call_last(place, mine, theirs, gain, far, before):
     tokens = mine[0].shape[0]
     rows = sum(b.shape[0] for b in before) + tokens // 32
     return local(
-        functools.partial(last_kernel, len(before)), [place],
-        [*mine, *theirs, gain, *weights, *before],
+        functools.partial(last_kernel, len(before)), [place], [*mine, *theirs, gain, *before],
         [out_vmem((16, rows, 256), f32), out_vmem((tokens // 32, 512), f32)],
-        mlp_scratch(tokens), "last_mlp",
+        [pltpu.VMEM((1, 4096, 640), bf16)] * 3
+        + [pltpu.SemaphoreType.DMA((12,))]
+        + mlp_scratch(tokens),
+        28, far,
     )
 
 
@@ -353,11 +386,14 @@
     chosen = chosen_ref[...]
     count = skew.shape[0]
     hot = (lax.broadcasted_iota(jnp.int32, (chosen.shape[0], count), 1) == chosen).astype(f32)
-    rows = jnp.dot(hot, skew, precision=lax.Precision.HIGHEST, preferred_element_type=f32)
-    out_ref[...] = lax.dot_general(
+    half = out_ref.shape[0]
+    rows = jnp.dot(hot[: 2 * half], skew, precision=lax.Precision.HIGHEST, preferred_element_type=f32)
+    tile = lax.dot_general(
         rows, hot, (((1,), (1,)), ((), ())),
         precision=lax.Precision.HIGHEST, preferred_element_type=f32,
     )
+    lane = lax.broadcasted_iota(jnp.int32, out_ref.shape, 1)
+    out_ref[...] = jnp.where(lane < half, tile[:half], tile[half:])
 
 
 def head_part(place, chosen, everyone, gain, head):
@@ -366,7 +402,7 @@
         head_kernel,
         in_specs=[pl.BlockSpec(memory_space=pltpu.SMEM)] + [vmem] * 4,
         out_specs=vmem,
-        out_shape=jax.ShapeDtypeStruct((chosen.shape[0], chosen.shape[0]), f32),
+        out_shape=jax.ShapeDtypeStruct((GROUP, chosen.shape[0]), f32),
         name="head",
     )(place, chosen, everyone, gain, head)
 
@@ -382,45 +418,59 @@
     place = jnp.stack([x, c, y, section]).astype(jnp.int32)
     ids = jnp.where(y == 0, token_ids, other_dp(token_ids))
     flat = ids.reshape(-1, 1) - section * embed_table.shape[1]
-    parts = embed_parts(flat, embed_table, BLOCKS)
-    weights = loaded(parts[0], gate_weight, up_weight, down_weight)
-    size = (parts[0].shape[0], 512)
-    half = (parts[0].shape[0], 256)
-
-    fresh = []
-    for part in parts:
-        pieces = [to_first(part, z) for z in (1, 3, 2)]
-        own = local(gathered_kernel, [], [part, *pieces], out_vmem(half, bf16), (), "gathered")
-        fresh.append((own, other_y(own)))
-    state = local(fresh_kernel, [place], fresh[0], out_vmem(size, bf16), (), "fresh")
+    together = flat.shape[0] * STREAMS // BLOCKS
+    rounds = BLOCKS // STREAMS
+    block = together // STREAMS
+    size = (block, 512)
+
+    def summed(part):
+        pieces = []
+        for z in (1, 3, 2):
+            pieces.append(along_sections(part, z))
+        return local(gathered_kernel, [], [part, *pieces], out_vmem(part.shape, bf16), ())
+
+    def start_of(own):
+        return local(fresh_kernel, [place], [own, other_y(own)], [out_vmem(size, bf16)], ())[0]
+
+    part = embed_part(place, flat, 0, together, embed_table)
+    own = summed(part)
+    weights = loaded(part, gate_weight, up_weight, down_weight)
+    state = start_of(own)
     sums_state, sums_hidden = [], []
-    ticks = BLOCKS + 3
+    ticks = rounds + 3
     for tick in range(ticks):
-        mine = [state] + [along_x(state, s) for s in (1, 3, 2)]
-        mine = [mine[i] for i in (0, 1, 3, 2)]
+        mine = [state]
+        for s in (1, 2, 3):
+            mine.append(along_x(state, s))
         theirs = [other_core(m) for m in mine]
         if tick == ticks - 1:
-            terms, base = call_last(place, mine, theirs, norm_gain, weights, sums_hidden)
+            far = (gate_weight, up_weight, down_weight)
+            terms, base = call_last(place, mine, theirs, norm_gain, far, sums_hidden)
             sums_state.append(base)
             break
         send, keep, *pooled = call_mlp(place, mine, theirs, norm_gain, weights, tick >= 3)
         if tick >= 3:
             sums_hidden.append(pooled[0])
             sums_state.append(pooled[1])
-        own, *halves = local(
+        own, *out = local(
             halves_kernel, [], [keep, other_core(send)],
-            [out_vmem(size, f32)] + [out_vmem(size, bf16)] * 3, (), "halves",
+            [out_vmem(size, f32)] + [out_vmem(size, bf16)] * 3, (),
         )
-        arrived = [along_x(halves[s - 1], s) for s in (1, 3, 2)]
-        total = local(
-            total_kernel, [place], [own, state, *arrived], out_vmem(size, bf16), (), "total"
-        )
-        ahead = [onward(total, 0), onward(total, 1)]
-        kernel = join_kernel
-        if tick + 1 < BLOCKS:
-            ahead += fresh[tick + 1]
-            kernel = join_fresh_kernel
-        state = local(kernel, [place], ahead, out_vmem(size, bf16), (), "join")
+        arrived = []
+        for s in (2, 1, 3):
+            arrived.append(along_x(out[s - 1], s))
+        if tick + 1 < rounds:
+            part = embed_part(place, flat, (tick + 1) * together, together, embed_table)
+        if tick + 1 < rounds:
+            fresh = start_of(summed(part))
+        total = local(total_kernel, [place], [own, state, *arrived], out_vmem(size, bf16), ())
+        ahead, kernel = [onward(total, 0), onward(total, 1)], join_kernel
+        if tick + 1 < rounds:
+            ahead, kernel = [*ahead, fresh], join_fresh_kernel
+        state = local(kernel, [place], ahead, out_vmem(size, bf16), ())
+    owners, members, final_gain, terms = lax.optimization_barrier(
+        (owners, members, final_gain, terms)
+    )
 
     groups = [[(g ^ ((m // 2) % 2)) * 16 + m for m in range(16)] for g in range(2)]
     pieces = lax.all_to_all(
@@ -440,19 +490,20 @@
     match = (owners[None, :] == slots[:, None]).astype(jnp.int32)
     hit = match[:, :, None] * members.reshape(prompts, GROUP)[None]
     chosen = jnp.sum(hit, axis=1).reshape(here * GROUP, 1)
+    chosen = jnp.pad(chosen, ((0, 128 - here * GROUP), (0, 0)), constant_values=-1)
     tile = head_part(
         jnp.reshape(mp, (1,)).astype(jnp.int32), chosen, everyone, final_gain[None], head_weight
     )
     rows = GROUP // 4
-    parts = jnp.stack(
-        [tile[p * GROUP : (p + 1) * GROUP, p * GROUP : (p + 1) * GROUP] for p in range(here)]
-    )
-    parts = jnp.swapaxes(parts.reshape(here, 4, rows, GROUP), 0, 1).reshape(4, here * rows, GROUP)
-    parts = jnp.pad(parts, ((0, 0), (0, 8 - here * rows), (0, 128 - GROUP)))
-    parts = jnp.broadcast_to(parts[None, :, None], (2, 4, 16, 8, 128)).reshape(128, 8, 128)
-    got = lax.all_to_all(parts, AXES, 0, 0, tiled=True).reshape(2, 4, 16, 8, 128)
-    skew = jnp.sum(jnp.where(dp == 0, got[0, 3], got[1, 3]), axis=0)[: here * rows, :GROUP]
-    return jax.nn.sigmoid(skew).reshape(here, rows, GROUP)
+    got = lax.all_to_all(
+        jnp.broadcast_to(tile, (16, GROUP, 128)), "mp", 0, 0, tiled=True
+    )
+    skew = jnp.sum(got, axis=0)
+    options = jnp.stack([along_sections(skew, (s + 1) % 4) for s in range(3)] + [skew])
+    skew = lax.dynamic_index_in_dim(options, section, 0, keepdims=False)
+    skew = lax.dynamic_slice_in_dim(skew, section * rows, rows, 0)
+    skew = jnp.stack([skew[:, p * GROUP : (p + 1) * GROUP] for p in range(here)])
+    return jax.nn.sigmoid(skew)
 
 
 def solution(mesh):
@@ -469,5 +520,6 @@
         P(None, "mp"),
     )
     return jax.shard_map(
-        per_device, mesh=mesh, in_specs=placed, out_specs=P("dp", "section", None), check_vma=False
-    )
+        per_device, mesh=mesh, in_specs=placed, out_specs=P("dp", "section", None),
+        check_vma=False,
+    )

time: 361 us -> 354 us (0.981)
  starting transfers between devices: 102 us -> 78.9 us
  waiting for transfers between devices: 170 us -> 181 us
  blocking collectives: 0 us -> 10.8 us
  local copies, waits for them, and re-layouts: 12.3 us -> 4.04 us
  Pallas kernels: 72 us -> 76.5 us
    ppermute x68 -> x71, waiting for transfers between devices: 141 us -> 165 us  [moved(): return lax.ppermute(value, AXES, pairs)]
    ppermute x68 -> x71, starting transfers between devices: 83.7 us -> 69.6 us  [moved(): return lax.ppermute(value, AXES, pairs)]
    all_to_all x1 -> x0, waiting for transfers between devices: 12.9 us -> none  [per_device(): lax.all_to_all(parts, AXES, 0, 0, tiled=True).reshape(2, 4, 16, 8, 128)]
    all_to_all x0 -> x1, blocking collectives: none -> 10.8 us  [per_device(): lax.all_to_all(jnp.broadcast_to(tile, (16, GROUP, 128)), 'mp', 0, 0, tile...]
    all_to_all x1 -> x0, starting transfers between devices: 8.87 us -> none  [per_device(): lax.all_to_all(parts, AXES, 0, 0, tiled=True).reshape(2, 4, 16, 8, 128)]
    unnamed x21 -> x9, local copies, waits for them, and re-layouts: 8.18 us -> 0.73 us
    pallas_call x1 -> x2, Pallas kernels: 11.9 us -> 17.1 us  [embed_part(): pl.pallas_call(functools.partial(embed_kernel, width, first), in_specs=[S...]
    pallas_call x20 -> x21, Pallas kernels: 51.2 us -> 50.2 us  [local(): pl.pallas_call(kernel, in_specs=[SMEM_SPEC] * len(scalars) + [VMEM_SPEC]...]
  transfers between devices with their start and end apart: 71 -> 73, of which waited for: 51 -> 45; matrix products, arithmetic and copies ran while one was open for 0% -> 1% of each run, Pallas kernels for 2% -> 4%
where the time goes in v1:
time: 354 us; the launch traced here: 353 us
  waiting for transfers between devices  181 us (51%)
  starting transfers between devices  78.9 us (22%)
  Pallas kernels  76.5 us (22%)
  blocking collectives  10.8 us (3%)
  local copies, waits for them, and re-layouts  4.04 us (1%)
    ppermute x71, waiting for transfers between devices, moved(): return lax.ppermute(value, AXES, pairs)  165 us
    ppermute x71, starting transfers between devices, moved(): return lax.ppermute(value, AXES, pairs)  69.6 us
    pallas_call x21, Pallas kernels, local(): pl.pallas_call(kernel, in_specs=[SMEM_SPEC] * len(scalars) + [VMEM_SPEC]...  50.2 us
    pallas_call x2, Pallas kernels, embed_part(): pl.pallas_call(functools.partial(embed_kernel, width, first), in_specs=[S...  17.1 us
    all_to_all x1, blocking collectives, per_device(): lax.all_to_all(jnp.broadcast_to(tile, (16, GROUP, 128)), 'mp', 0, 0, tile...  10.8 us
    all_to_all x1, waiting for transfers between devices, per_device(): lax.all_to_all(jnp.broadcast_to(value, (32, *value.shape)), ('dp', 'mp'),...  8.03 us
    all_to_all x1, waiting for transfers between devices, per_device(): lax.all_to_all(terms, ('dp', 'mp'), 0, 0, tiled=True, axis_index_groups=g...  7.99 us
  transfers between devices with their start and end apart: 73, of which 45 were waited for; matrix products, arithmetic and copies ran while one was open for 1% of the time, Pallas kernels for 4%

profile of v1, /device:TPU:0, one launch (start us, length us, event | category | flops | bytes accessed | tf_op | source)
XLA Modules:
  0.0 353.1 jit_solution(14944081360306309280)
XLA Ops:
  4.8 8.6 %embed.2.own.after = bf16[256,256]{1,0:T(8,128)(2,1)S(1)} custom-call(s32[4]{0:T(128)S(1)} %pad_add_fusion.place.flag, s32[512,1]{1,0:T(8,128)S(1)} %sub.20.ids_ref, bf16[256,16384]{1,0:T(8,128)(2,1)} %table_ref.3), custom_call_target="tpu_custom_call" | custom-call | flops 2147483648 | tf_op jit(solution)/shard_map/embed/pallas_call | solution.py:110
  26.9 3.9 %collective-permute-done.4.peer = bf16[256,256]{1,0:T(8,128)(2,1)S(1)} collective-permute-done((bf16[256,256]{1,0:T(8,128)(2,1)S(1)}, bf16[256,256]{1,0:T(8,128)(2,1)S(1)}, u32[]{:S(2)}, u32[]{:S(2)}) %collective-permute-start.4) | collective-permute-done | bytes 131104 | tf_op jit(solution)/shard_map/ppermute | solution.py:35
  31.4 3.1 collective-permute-start.6
  36.5 4.4 %collective-permute-done.6.refs_2_ = bf16[256,512]{1,0:T(8,128)(2,1)S(1)} collective-permute-done((bf16[256,512]{1,0:T(8,128)(2,1)S(1)}, bf16[256,512]{1,0:T(8,128)(2,1)S(1)}, u32[]{:S(2)}, u32[]{:S(2)}) %collective-permute-start.6) | collective-permute-done | bytes 262176 | tf_op jit(solution)/shard_map/ppermute | solution.py:35
  40.9 2.9 collective-permute-done.7.refs_3_
  44.3 5.6 %load.1 = (bf16[1,4096,640]{2,1,0:T(8,128)(2,1)S(1)}, bf16[1,4096,640]{2,1,0:T(8,128)(2,1)S(1)}, bf16[1,4096,640]{2,1,0:T(8,128)(2,1)S(1)}) custom-call(bf16[256,256]{1,0:T(8,128)(2,1)S(1)} %embed.2.own.after, bf16[1,4096,640]{2,1,0:T(8,128)(2,1)} %refs_10_.1, bf16[1,4096,640]{2,1,0:T(8,128)(2,1)} %refs_11_.1, bf16[1,4096,640]{2,1,0:T(8,128)(2,1)} %refs_12_.1), custom_call_target="tpu_custom_call" | custom-call | tf_op jit(solution)/shard_map/load/pallas_call | solution.py:143
  50.0 8.3 %shard_map.102 = (bf16[4,256,512]{2,1,0:T(8,128)(2,1)S(1)}, bf16[4,256,512]{2,1,0:T(8,128)(2,1)S(1)}) custom-call(s32[4]{0:T(128)S(1)} %pad_add_fusion.place.flag, bf16[256,512]{1,0:T(8,128)(2,1)S(1)} %shard_map.101.refs_0_.state, bf16[256,512]{1,0:T(8,128)(2,1)S(1)} %collective-permute-done.5.refs_1_, bf16[256,512]{1,0:T(8,128)(2,1)S(1)} %collective-permute-done.6.refs_2_, ...), custom_call_target="tpu_custom_call" | custom-call | tf_op jit(solution)/shard_map/pallas_call | solution.py:317
  61.3 2.6 collective-permute-start.13
  67.1 8.6 %embed.3.own = bf16[256,256]{1,0:T(8,128)(2,1)S(1)} custom-call(s32[4]{0:T(128)S(1)} %pad_add_fusion.place.flag, s32[512,1]{1,0:T(8,128)S(1)} %sub.20.ids_ref, bf16[256,16384]{1,0:T(8,128)(2,1)} %table_ref.3), custom_call_target="tpu_custom_call" | custom-call | flops 2147483648 | tf_op jit(solution)/shard_map/embed/pallas_call | solution.py:110
  75.7 3.2 collective-permute-start.19
  81.5 3.5 %collective-permute-start.17 = (bf16[256,512]{1,0:T(8,128)(2,1)S(1)}, bf16[256,512]{1,0:T(8,128)(2,1)S(1)}, u32[]{:S(2)}, u32[]{:S(2)}) collective-permute-start(bf16[256,512]{1,0:T(8,128)(2,1)S(1)} %shard_map.104), channel_id=1, source_target_pairs={{0,82},{1,83},{2,80},{3,81},{4,86},{5,87},{6,84},{7,85},{8,90},{9,... | collective-permute-start | bytes 786440 | tf_op jit(solution)/shard_map/ppermute | solution.py:35
  85.0 5.9 %collective-permute-done.20.d = bf16[256,256]{1,0:T(8,128)(2,1)S(1)} collective-permute-done((bf16[256,256]{1,0:T(8,128)(2,1)S(1)}, bf16[256,256]{1,0:T(8,128)(2,1)S(1)}, u32[]{:S(2)}, u32[]{:S(2)}) %collective-permute-start.20) | collective-permute-done | bytes 131104 | tf_op jit(solution)/shard_map/ppermute | solution.py:35
  93.4 3.9 %collective-permute-done.21.peer = bf16[256,256]{1,0:T(8,128)(2,1)S(1)} collective-permute-done((bf16[256,256]{1,0:T(8,128)(2,1)S(1)}, bf16[256,256]{1,0:T(8,128)(2,1)S(1)}, u32[]{:S(2)}, u32[]{:S(2)}) %collective-permute-start.21) | collective-permute-done | bytes 131104 | tf_op jit(solution)/shard_map/ppermute | solution.py:35
  98.8 3.0 collective-permute-start.24
  101.8 9.7 %collective-permute-done.22.refs_1_ = bf16[256,512]{1,0:T(8,128)(2,1)S(1)} collective-permute-done((bf16[256,512]{1,0:T(8,128)(2,1)S(1)}, bf16[256,512]{1,0:T(8,128)(2,1)S(1)}, u32[]{:S(2)}, u32[]{:S(2)}) %collective-permute-start.22) | collective-permute-done | bytes 262176 | tf_op jit(solution)/shard_map/ppermute | solution.py:35
  113.8 8.3 %shard_map.108 = (bf16[4,256,512]{2,1,0:T(8,128)(2,1)S(1)}, bf16[4,256,512]{2,1,0:T(8,128)(2,1)S(1)}) custom-call(s32[4]{0:T(128)S(1)} %pad_add_fusion.place.flag, bf16[256,512]{1,0:T(8,128)(2,1)S(1)} %shard_map.107.refs_0_.state, bf16[256,512]{1,0:T(8,128)(2,1)S(1)} %collective-permute-done.22.refs_1_, ...), custom_call_target="tpu_custom_call" | custom-call | tf_op jit(solution)/shard_map/pallas_call | solution.py:317
  122.3 2.5 collective-permute-done.29.got
  128.9 7.0 %collective-permute-done.30.a = bf16[256,512]{1,0:T(8,128)(2,1)S(1)} collective-permute-done((bf16[256,512]{1,0:T(8,128)(2,1)S(1)}, bf16[256,512]{1,0:T(8,128)(2,1)S(1)}, u32[]{:S(2)}, u32[]{:S(2)}) %collective-permute-start.30) | collective-permute-done | bytes 262176 | tf_op jit(solution)/shard_map/ppermute | solution.py:35
  135.9 4.6 %collective-permute-done.31.b = bf16[256,512]{1,0:T(8,128)(2,1)S(1)} collective-permute-done((bf16[256,512]{1,0:T(8,128)(2,1)S(1)}, bf16[256,512]{1,0:T(8,128)(2,1)S(1)}, u32[]{:S(2)}, u32[]{:S(2)}) %collective-permute-start.31) | collective-permute-done | bytes 262176 | tf_op jit(solution)/shard_map/ppermute | solution.py:35
  143.4 12.8 %collective-permute-done.33.a = bf16[256,512]{1,0:T(8,128)(2,1)S(1)} collective-permute-done((bf16[256,512]{1,0:T(8,128)(2,1)S(1)}, bf16[256,512]{1,0:T(8,128)(2,1)S(1)}, u32[]{:S(2)}, u32[]{:S(2)}) %collective-permute-start.33) | collective-permute-done | bytes 262176 | tf_op jit(solution)/shard_map/ppermute | solution.py:35
  157.0 3.6 %collective-permute-start.36 = (bf16[256,512]{1,0:T(8,128)(2,1)S(1)}, bf16[256,512]{1,0:T(8,128)(2,1)S(1)}, u32[]{:S(2)}, u32[]{:S(2)}) collective-permute-start(bf16[256,512]{1,0:T(8,128)(2,1)S(1)} %shard_map.111.refs_0_.state), channel_id=1, source_target_pairs={{0,8},{1,9},{2,10},{3,11},{4,12},{5,13},{6,14},{7,15},{8,0},{9,1},... | collective-permute-start | bytes 786440 | tf_op jit(solution)/shard_map/ppermute | solution.py:35
  160.6 6.1 %collective-permute-done.35.refs_1_ = bf16[256,512]{1,0:T(8,128)(2,1)S(1)} collective-permute-done((bf16[256,512]{1,0:T(8,128)(2,1)S(1)}, bf16[256,512]{1,0:T(8,128)(2,1)S(1)}, u32[]{:S(2)}, u32[]{:S(2)}) %collective-permute-start.35) | collective-permute-done | bytes 262176 | tf_op jit(solution)/shard_map/ppermute | solution.py:35
  166.7 4.9 %collective-permute-done.36.refs_2_ = bf16[256,512]{1,0:T(8,128)(2,1)S(1)} collective-permute-done((bf16[256,512]{1,0:T(8,128)(2,1)S(1)}, bf16[256,512]{1,0:T(8,128)(2,1)S(1)}, u32[]{:S(2)}, u32[]{:S(2)}) %collective-permute-start.36) | collective-permute-done | bytes 262176 | tf_op jit(solution)/shard_map/ppermute | solution.py:35
  173.4 8.3 %shard_map.112 = (bf16[4,256,512]{2,1,0:T(8,128)(2,1)S(1)}, bf16[4,256,512]{2,1,0:T(8,128)(2,1)S(1)}) custom-call(s32[4]{0:T(128)S(1)} %pad_add_fusion.place.flag, bf16[256,512]{1,0:T(8,128)(2,1)S(1)} %shard_map.111.refs_0_.state, bf16[256,512]{1,0:T(8,128)(2,1)S(1)} %collective-permute-done.35.refs_1_, ...), custom_call_target="tpu_custom_call" | custom-call | tf_op jit(solution)/shard_map/pallas_call | solution.py:317
  182.0 2.5 collective-permute-done.42.got
  185.4 2.6 collective-permute-start.44
  188.7 6.9 %collective-permute-done.43.a = bf16[256,512]{1,0:T(8,128)(2,1)S(1)} collective-permute-done((bf16[256,512]{1,0:T(8,128)(2,1)S(1)}, bf16[256,512]{1,0:T(8,128)(2,1)S(1)}, u32[]{:S(2)}, u32[]{:S(2)}) %collective-permute-start.43) | collective-permute-done | bytes 262176 | tf_op jit(solution)/shard_map/ppermute | solution.py:35
  195.5 4.7 %collective-permute-done.44.b = bf16[256,512]{1,0:T(8,128)(2,1)S(1)} collective-permute-done((bf16[256,512]{1,0:T(8,128)(2,1)S(1)}, bf16[256,512]{1,0:T(8,128)(2,1)S(1)}, u32[]{:S(2)}, u32[]{:S(2)}) %collective-permute-start.44) | collective-permute-done | bytes 262176 | tf_op jit(solution)/shard_map/ppermute | solution.py:35
  202.3 13.9 %collective-permute-done.46.a = bf16[256,512]{1,0:T(8,128)(2,1)S(1)} collective-permute-done((bf16[256,512]{1,0:T(8,128)(2,1)S(1)}, bf16[256,512]{1,0:T(8,128)(2,1)S(1)}, u32[]{:S(2)}, u32[]{:S(2)}) %collective-permute-start.46) | collective-permute-done | bytes 262176 | tf_op jit(solution)/shard_map/ppermute | solution.py:35
  216.8 3.8 %collective-permute-start.49 = (bf16[256,512]{1,0:T(8,128)(2,1)S(1)}, bf16[256,512]{1,0:T(8,128)(2,1)S(1)}, u32[]{:S(2)}, u32[]{:S(2)}) collective-permute-start(bf16[256,512]{1,0:T(8,128)(2,1)S(1)} %shard_map.115.refs_0_.state), channel_id=1, source_target_pairs={{0,8},{1,9},{2,10},{3,11},{4,12},{5,13},{6,14},{7,15},{8,0},{9,1},... | collective-permute-start | bytes 786440 | tf_op jit(solution)/shard_map/ppermute | solution.py:35
  220.6 6.0 %collective-permute-done.48.refs_1_ = bf16[256,512]{1,0:T(8,128)(2,1)S(1)} collective-permute-done((bf16[256,512]{1,0:T(8,128)(2,1)S(1)}, bf16[256,512]{1,0:T(8,128)(2,1)S(1)}, u32[]{:S(2)}, u32[]{:S(2)}) %collective-permute-start.48) | collective-permute-done | bytes 262176 | tf_op jit(solution)/shard_map/ppermute | solution.py:35
  226.6 5.0 %collective-permute-done.49.refs_2_ = bf16[256,512]{1,0:T(8,128)(2,1)S(1)} collective-permute-done((bf16[256,512]{1,0:T(8,128)(2,1)S(1)}, bf16[256,512]{1,0:T(8,128)(2,1)S(1)}, u32[]{:S(2)}, u32[]{:S(2)}) %collective-permute-start.49) | collective-permute-done | bytes 262176 | tf_op jit(solution)/shard_map/ppermute | solution.py:35
  233.5 8.4 %shard_map.116 = (bf16[4,256,512]{2,1,0:T(8,128)(2,1)S(1)}, bf16[4,256,512]{2,1,0:T(8,128)(2,1)S(1)}, f32[8,640]{1,0:T(8,128)S(1)}, f32[8,512]{1,0:T(8,128)S(1)}) custom-call(s32[4]{0:T(128)S(1)} %pad_add_fusion.place.flag, bf16[256,512]{1,0:T(8,128)(2,1)S(1)} %shard_map.115.refs_0_.state, bf16[256,512]{1,0:T(8,128)(2,1)S(1)} %collective-permute-done.48.refs_1_, ...), custom_call_target="tpu_custom_call" | custom-call | tf_op jit(solution)/shard_map/pallas_call | solution.py:317
  242.1 2.5 collective-permute-done.55.got
  245.5 2.6 collective-permute-start.57
  248.8 6.9 %collective-permute-done.56.a = bf16[256,512]{1,0:T(8,128)(2,1)S(1)} collective-permute-done((bf16[256,512]{1,0:T(8,128)(2,1)S(1)}, bf16[256,512]{1,0:T(8,128)(2,1)S(1)}, u32[]{:S(2)}, u32[]{:S(2)}) %collective-permute-start.56) | collective-permute-done | bytes 262176 | tf_op jit(solution)/shard_map/ppermute | solution.py:35
  255.7 4.7 %collective-permute-done.57.b = bf16[256,512]{1,0:T(8,128)(2,1)S(1)} collective-permute-done((bf16[256,512]{1,0:T(8,128)(2,1)S(1)}, bf16[256,512]{1,0:T(8,128)(2,1)S(1)}, u32[]{:S(2)}, u32[]{:S(2)}) %collective-permute-start.57) | collective-permute-done | bytes 262176 | tf_op jit(solution)/shard_map/ppermute | solution.py:35
  262.4 13.8 %collective-permute-done.59.a = bf16[256,512]{1,0:T(8,128)(2,1)S(1)} collective-permute-done((bf16[256,512]{1,0:T(8,128)(2,1)S(1)}, bf16[256,512]{1,0:T(8,128)(2,1)S(1)}, u32[]{:S(2)}, u32[]{:S(2)}) %collective-permute-start.59) | collective-permute-done | bytes 262176 | tf_op jit(solution)/shard_map/ppermute | solution.py:35
  277.0 3.8 %collective-permute-start.62 = (bf16[256,512]{1,0:T(8,128)(2,1)S(1)}, bf16[256,512]{1,0:T(8,128)(2,1)S(1)}, u32[]{:S(2)}, u32[]{:S(2)}) collective-permute-start(bf16[256,512]{1,0:T(8,128)(2,1)S(1)} %shard_map.119.refs_0_), channel_id=1, source_target_pairs={{0,8},{1,9},{2,10},{3,11},{4,12},{5,13},{6,14},{7,15},{8,0},{9,1},... | collective-permute-start | bytes 786440 | tf_op jit(solution)/shard_map/ppermute | solution.py:35
  280.7 6.0 %collective-permute-done.61.refs_1_ = bf16[256,512]{1,0:T(8,128)(2,1)S(1)} collective-permute-done((bf16[256,512]{1,0:T(8,128)(2,1)S(1)}, bf16[256,512]{1,0:T(8,128)(2,1)S(1)}, u32[]{:S(2)}, u32[]{:S(2)}) %collective-permute-start.61) | collective-permute-done | bytes 262176 | tf_op jit(solution)/shard_map/ppermute | solution.py:35
  286.8 4.9 %collective-permute-done.62.refs_2_ = bf16[256,512]{1,0:T(8,128)(2,1)S(1)} collective-permute-done((bf16[256,512]{1,0:T(8,128)(2,1)S(1)}, bf16[256,512]{1,0:T(8,128)(2,1)S(1)}, u32[]{:S(2)}, u32[]{:S(2)}) %collective-permute-start.62) | collective-permute-done | bytes 262176 | tf_op jit(solution)/shard_map/ppermute | solution.py:35
  293.6 9.4 %shard_map.120 = (f32[16,16,256]{2,1,0:T(8,128)}, f32[8,512]{1,0:T(8,128)S(1)}) custom-call(s32[4]{0:T(128)S(1)} %pad_add_fusion.place.flag, bf16[256,512]{1,0:T(8,128)(2,1)S(1)} %shard_map.119.refs_0_, bf16[256,512]{1,0:T(8,128)(2,1)S(1)} %collective-permute-done.61.refs_1_, bf16[256,512]{1,0:T(8,128)(2,1)S(1)} %collective-permute-done.62.refs_2_, ...), custom_call_target="tpu_custom_call" | custom-call | tf_op jit(solution)/shard_map/pallas_call | solution.py:317
  303.0 5.5 %all-to-all-start = ((f32[16,16,256]{2,1,0:T(8,128)}), f32[16,16,256]{2,1,0:T(8,128)S(1)}, u32[]{:S(2)}, u32[]{:S(2)}) async-start(f32[16,16,256]{2,1,0:T(8,128)} %get-tuple-element.71), calls=%async_computation | async-start | bytes 524288 | tf_op jit(solution)/shard_map/all_to_all | solution.py:476
  309.4 8.0 %all-to-all-done = f32[16,16,256]{2,1,0:T(8,128)S(1)} async-done(((f32[16,16,256]{2,1,0:T(8,128)}), f32[16,16,256]{2,1,0:T(8,128)S(1)}, u32[]{:S(2)}, u32[]{:S(2)}) %all-to-all-start) | async-done | bytes 262176 | tf_op jit(solution)/shard_map/all_to_all | solution.py:476
  318.2 3.9 %all-to-all-start.1 = ((bf16[32,16,256]{2,1,0:T(8,128)(2,1)}), bf16[32,16,256]{2,1,0:T(8,128)(2,1)S(1)}, u32[]{:S(2)}, u32[]{:S(2)}) async-start(bf16[32,16,256]{2,1,0:T(8,128)(2,1)} %broadcast_in_dim.6), calls=%async_computation.1 | async-start | bytes 524288 | tf_op jit(solution)/shard_map/all_to_all | solution.py:483
  322.9 8.0 %all-to-all-done.1 = bf16[32,16,256]{2,1,0:T(8,128)(2,1)S(1)} async-done(((bf16[32,16,256]{2,1,0:T(8,128)(2,1)}), bf16[32,16,256]{2,1,0:T(8,128)(2,1)S(1)}, u32[]{:S(2)}, u32[]{:S(2)}) %all-to-all-start.1) | async-done | bytes 262176 | tf_op jit(solution)/shard_map/all_to_all | solution.py:483
  331.7 3.5 head.1
  335.9 10.8 %all_to_all.15 = f32[16,8,128]{2,1,0:T(8,128)S(1)} all-to-all(f32[16,8,128]{2,1,0:T(8,128)S(1)} %broadcast_in_dim.15), channel_id=1, replica_groups=mesh['dp'=2,'section'=4,'mp'=16] {'mp'}, dimensions={0} | all-to-all | bytes 131072 | tf_op jit(solution)/shard_map/all_to_all | solution.py:498
  (152 shorter events, 69.3 us)
Async XLA Ops:
  13.4 7.9 %collective-permute-start.1 = (bf16[256,256]{1,0:T(8,128)(2,1)S(1)}, bf16[256,256]{1,0:T(8,128)(2,1)S(1)}, u32[]{:S(2)}, u32[]{:S(2)}) collective-permute-start(bf16[256,256]{1,0:T(8,128)(2,1)S(1)} %embed.2.own.after), channel_id=1, source_target_pairs={{0,16},{1,17},{2,18},{3,19},{4,20},{5,21},{6,22},{7,23},{8,24},{9,... | collective-permute-start | bytes 393224 | tf_op jit(solution)/shard_map/ppermute | solution.py:35
  15.5 7.2 %collective-permute-start.2 = (bf16[256,256]{1,0:T(8,128)(2,1)S(1)}, bf16[256,256]{1,0:T(8,128)(2,1)S(1)}, u32[]{:S(2)}, u32[]{:S(2)}) collective-permute-start(bf16[256,256]{1,0:T(8,128)(2,1)S(1)} %embed.2.own.after), channel_id=1, source_target_pairs={{0,48},{1,49},{2,50},{3,51},{4,52},{5,53},{6,54},{7,55},{8,56},{9,... | collective-permute-start | bytes 393224 | tf_op jit(solution)/shard_map/ppermute | solution.py:35
  31.4 9.6 %collective-permute-start.6 = (bf16[256,512]{1,0:T(8,128)(2,1)S(1)}, bf16[256,512]{1,0:T(8,128)(2,1)S(1)}, u32[]{:S(2)}, u32[]{:S(2)}) collective-permute-start(bf16[256,512]{1,0:T(8,128)(2,1)S(1)} %shard_map.101.refs_0_.state), channel_id=1, source_target_pairs={{0,8},{1,9},{2,10},{3,11},{4,12},{5,13},{6,14},{7,15},{8,0},{9,1},... | collective-permute-start | bytes 786440 | tf_op jit(solution)/shard_map/ppermute | solution.py:35
  34.5 9.3 %collective-permute-start.7 = (bf16[256,512]{1,0:T(8,128)(2,1)S(1)}, bf16[256,512]{1,0:T(8,128)(2,1)S(1)}, u32[]{:S(2)}, u32[]{:S(2)}) collective-permute-start(bf16[256,512]{1,0:T(8,128)(2,1)S(1)} %shard_map.101.refs_0_.state), channel_id=1, source_target_pairs={{0,12},{1,13},{2,14},{3,15},{4,0},{5,1},{6,2},{7,3},{8,4},{9,5},{1... | collective-permute-start | bytes 786440 | tf_op jit(solution)/shard_map/ppermute | solution.py:35
  35.6 8.5 %collective-permute-start.5 = (bf16[256,512]{1,0:T(8,128)(2,1)S(1)}, bf16[256,512]{1,0:T(8,128)(2,1)S(1)}, u32[]{:S(2)}, u32[]{:S(2)}) collective-permute-start(bf16[256,512]{1,0:T(8,128)(2,1)S(1)} %shard_map.101.refs_0_.state), channel_id=1, source_target_pairs={{0,4},{1,5},{2,6},{3,7},{4,8},{5,9},{6,10},{7,11},{8,12},{9,13},{1... | collective-permute-start | bytes 786440 | tf_op jit(solution)/shard_map/ppermute | solution.py:35
  36.5 13.4 %collective-permute-start.8 = (bf16[256,512]{1,0:T(8,128)(2,1)S(1)}, bf16[256,512]{1,0:T(8,128)(2,1)S(1)}, u32[]{:S(2)}, u32[]{:S(2)}) collective-permute-start(bf16[256,512]{1,0:T(8,128)(2,1)S(1)} %shard_map.101.refs_0_.state), channel_id=1, source_target_pairs={{0,1},{1,0},{2,3},{3,2},{4,5},{5,4},{6,7},{7,6},{8,9},{9,8},{10,11... | collective-permute-start | bytes 786440 | tf_op jit(solution)/shard_map/ppermute | solution.py:35
  40.9 9.0 %collective-permute-start.10 = (bf16[256,512]{1,0:T(8,128)(2,1)S(1)}, bf16[256,512]{1,0:T(8,128)(2,1)S(1)}, u32[]{:S(2)}, u32[]{:S(2)}) collective-permute-start(bf16[256,512]{1,0:T(8,128)(2,1)S(1)} %collective-permute-done.6.refs_2_), channel_id=1, source_target_pairs={{0,1},{1,0},{2,3},{3,2},{4,5},{5,4},{6,7},{7,6},{8,9},{9,8},{10,11... | collective-permute-start | bytes 786440 | tf_op jit(solution)/shard_map/ppermute | solution.py:35
  61.3 17.7 %collective-permute-start.13 = (bf16[256,512]{1,0:T(8,128)(2,1)S(1)}, bf16[256,512]{1,0:T(8,128)(2,1)S(1)}, u32[]{:S(2)}, u32[]{:S(2)}) collective-permute-start(bf16[256,512]{1,0:T(8,128)(2,1)S(1)} %get-tuple-element.46), channel_id=1, source_target_pairs={{0,8},{1,9},{2,10},{3,11},{4,12},{5,13},{6,14},{7,15},{8,0},{9,1},... | collective-permute-start | bytes 786440 | tf_op jit(solution)/shard_map/ppermute | solution.py:35
  63.8 15.4 %collective-permute-start.14 = (bf16[256,512]{1,0:T(8,128)(2,1)S(1)}, bf16[256,512]{1,0:T(8,128)(2,1)S(1)}, u32[]{:S(2)}, u32[]{:S(2)}) collective-permute-start(bf16[256,512]{1,0:T(8,128)(2,1)S(1)} %get-tuple-element.47), channel_id=1, source_target_pairs={{0,4},{1,5},{2,6},{3,7},{4,8},{5,9},{6,10},{7,11},{8,12},{9,13},{1... | collective-permute-start | bytes 786440 | tf_op jit(solution)/shard_map/ppermute | solution.py:35
  64.8 14.5 %collective-permute-start.15 = (bf16[256,512]{1,0:T(8,128)(2,1)S(1)}, bf16[256,512]{1,0:T(8,128)(2,1)S(1)}, u32[]{:S(2)}, u32[]{:S(2)}) collective-permute-start(bf16[256,512]{1,0:T(8,128)(2,1)S(1)} %get-tuple-element.48), channel_id=1, source_target_pairs={{0,12},{1,13},{2,14},{3,15},{4,0},{5,1},{6,2},{7,3},{8,4},{9,5},{1... | collective-permute-start | bytes 786440 | tf_op jit(solution)/shard_map/ppermute | solution.py:35
  75.7 9.3 %collective-permute-start.18 = (bf16[256,256]{1,0:T(8,128)(2,1)S(1)}, bf16[256,256]{1,0:T(8,128)(2,1)S(1)}, u32[]{:S(2)}, u32[]{:S(2)}) collective-permute-start(bf16[256,256]{1,0:T(8,128)(2,1)S(1)} %embed.3.own), channel_id=1, source_target_pairs={{0,16},{1,17},{2,18},{3,19},{4,20},{5,21},{6,22},{7,23},{8,24},{9,... | collective-permute-start | bytes 393224 | tf_op jit(solution)/shard_map/ppermute | solution.py:35
  75.7 9.3 %collective-permute-start.19 = (bf16[256,256]{1,0:T(8,128)(2,1)S(1)}, bf16[256,256]{1,0:T(8,128)(2,1)S(1)}, u32[]{:S(2)}, u32[]{:S(2)}) collective-permute-start(bf16[256,256]{1,0:T(8,128)(2,1)S(1)} %embed.3.own), channel_id=1, source_target_pairs={{0,48},{1,49},{2,50},{3,51},{4,52},{5,53},{6,54},{7,55},{8,56},{9,... | collective-permute-start | bytes 393224 | tf_op jit(solution)/shard_map/ppermute | solution.py:35
  79.0 11.9 %collective-permute-start.20 = (bf16[256,256]{1,0:T(8,128)(2,1)S(1)}, bf16[256,256]{1,0:T(8,128)(2,1)S(1)}, u32[]{:S(2)}, u32[]{:S(2)}) collective-permute-start(bf16[256,256]{1,0:T(8,128)(2,1)S(1)} %embed.3.own), channel_id=1, source_target_pairs={{0,32},{1,33},{2,34},{3,35},{4,36},{5,37},{6,38},{7,39},{8,40},{9,... | collective-permute-start | bytes 393224 | tf_op jit(solution)/shard_map/ppermute | solution.py:35
  80.0 17.9 %collective-permute-start.16 = (bf16[256,512]{1,0:T(8,128)(2,1)S(1)}, bf16[256,512]{1,0:T(8,128)(2,1)S(1)}, u32[]{:S(2)}, u32[]{:S(2)}) collective-permute-start(bf16[256,512]{1,0:T(8,128)(2,1)S(1)} %shard_map.104), channel_id=1, source_target_pairs={{0,16},{1,17},{2,18},{3,19},{4,20},{5,21},{6,22},{7,23},{8,24},{9,... | collective-permute-start | bytes 786440 | tf_op jit(solution)/shard_map/ppermute | solution.py:35
  81.5 16.4 %collective-permute-start.17 = (bf16[256,512]{1,0:T(8,128)(2,1)S(1)}, bf16[256,512]{1,0:T(8,128)(2,1)S(1)}, u32[]{:S(2)}, u32[]{:S(2)}) collective-permute-start(bf16[256,512]{1,0:T(8,128)(2,1)S(1)} %shard_map.104), channel_id=1, source_target_pairs={{0,82},{1,83},{2,80},{3,81},{4,86},{5,87},{6,84},{7,85},{8,90},{9,... | collective-permute-start | bytes 786440 | tf_op jit(solution)/shard_map/ppermute | solution.py:35
  98.5 13.0 %collective-permute-start.22 = (bf16[256,512]{1,0:T(8,128)(2,1)S(1)}, bf16[256,512]{1,0:T(8,128)(2,1)S(1)}, u32[]{:S(2)}, u32[]{:S(2)}) collective-permute-start(bf16[256,512]{1,0:T(8,128)(2,1)S(1)} %shard_map.107.refs_0_.state), channel_id=1, source_target_pairs={{0,4},{1,5},{2,6},{3,7},{4,8},{5,9},{6,10},{7,11},{8,12},{9,13},{1... | collective-permute-start | bytes 786440 | tf_op jit(solution)/shard_map/ppermute | solution.py:35
  98.6 12.9 %collective-permute-start.23 = (bf16[256,512]{1,0:T(8,128)(2,1)S(1)}, bf16[256,512]{1,0:T(8,128)(2,1)S(1)}, u32[]{:S(2)}, u32[]{:S(2)}) collective-permute-start(bf16[256,512]{1,0:T(8,128)(2,1)S(1)} %shard_map.107.refs_0_.state), channel_id=1, source_target_pairs={{0,8},{1,9},{2,10},{3,11},{4,12},{5,13},{6,14},{7,15},{8,0},{9,1},... | collective-permute-start | bytes 786440 | tf_op jit(solution)/shard_map/ppermute | solution.py:35
  98.8 13.2 %collective-permute-start.24 = (bf16[256,512]{1,0:T(8,128)(2,1)S(1)}, bf16[256,512]{1,0:T(8,128)(2,1)S(1)}, u32[]{:S(2)}, u32[]{:S(2)}) collective-permute-start(bf16[256,512]{1,0:T(8,128)(2,1)S(1)} %shard_map.107.refs_0_.state), channel_id=1, source_target_pairs={{0,12},{1,13},{2,14},{3,15},{4,0},{5,1},{6,2},{7,3},{8,4},{9,5},{1... | collective-permute-start | bytes 786440 | tf_op jit(solution)/shard_map/ppermute | solution.py:35
  101.8 10.3 %collective-permute-start.25 = (bf16[256,512]{1,0:T(8,128)(2,1)S(1)}, bf16[256,512]{1,0:T(8,128)(2,1)S(1)}, u32[]{:S(2)}, u32[]{:S(2)}) collective-permute-start(bf16[256,512]{1,0:T(8,128)(2,1)S(1)} %shard_map.107.refs_0_.state), channel_id=1, source_target_pairs={{0,1},{1,0},{2,3},{3,2},{4,5},{5,4},{6,7},{7,6},{8,9},{9,8},{10,11... | collective-permute-start | bytes 786440 | tf_op jit(solution)/shard_map/ppermute | solution.py:35
  125.1 10.8 %collective-permute-start.30 = (bf16[256,512]{1,0:T(8,128)(2,1)S(1)}, bf16[256,512]{1,0:T(8,128)(2,1)S(1)}, u32[]{:S(2)}, u32[]{:S(2)}) collective-permute-start(bf16[256,512]{1,0:T(8,128)(2,1)S(1)} %get-tuple-element.52), channel_id=1, source_target_pairs={{0,8},{1,9},{2,10},{3,11},{4,12},{5,13},{6,14},{7,15},{8,0},{9,1},... | collective-permute-start | bytes 786440 | tf_op jit(solution)/shard_map/ppermute | solution.py:35
  125.6 14.9 %collective-permute-start.31 = (bf16[256,512]{1,0:T(8,128)(2,1)S(1)}, bf16[256,512]{1,0:T(8,128)(2,1)S(1)}, u32[]{:S(2)}, u32[]{:S(2)}) collective-permute-start(bf16[256,512]{1,0:T(8,128)(2,1)S(1)} %get-tuple-element.53), channel_id=1, source_target_pairs={{0,4},{1,5},{2,6},{3,7},{4,8},{5,9},{6,10},{7,11},{8,12},{9,13},{1... | collective-permute-start | bytes 786440 | tf_op jit(solution)/shard_map/ppermute | solution.py:35
  128.0 12.6 %collective-permute-start.32 = (bf16[256,512]{1,0:T(8,128)(2,1)S(1)}, bf16[256,512]{1,0:T(8,128)(2,1)S(1)}, u32[]{:S(2)}, u32[]{:S(2)}) collective-permute-start(bf16[256,512]{1,0:T(8,128)(2,1)S(1)} %get-tuple-element.54), channel_id=1, source_target_pairs={{0,12},{1,13},{2,14},{3,15},{4,0},{5,1},{6,2},{7,3},{8,4},{9,5},{1... | collective-permute-start | bytes 786440 | tf_op jit(solution)/shard_map/ppermute | solution.py:35
  141.2 15.0 %collective-permute-start.33 = (bf16[256,512]{1,0:T(8,128)(2,1)S(1)}, bf16[256,512]{1,0:T(8,128)(2,1)S(1)}, u32[]{:S(2)}, u32[]{:S(2)}) collective-permute-start(bf16[256,512]{1,0:T(8,128)(2,1)S(1)} %shard_map.110), channel_id=1, source_target_pairs={{0,16},{1,17},{2,18},{3,19},{4,20},{5,21},{6,22},{7,23},{8,24},{9,... | collective-permute-start | bytes 786440 | tf_op jit(solution)/shard_map/ppermute | solution.py:35
  141.3 14.9 %collective-permute-start.34 = (bf16[256,512]{1,0:T(8,128)(2,1)S(1)}, bf16[256,512]{1,0:T(8,128)(2,1)S(1)}, u32[]{:S(2)}, u32[]{:S(2)}) collective-permute-start(bf16[256,512]{1,0:T(8,128)(2,1)S(1)} %shard_map.110), channel_id=1, source_target_pairs={{0,82},{1,83},{2,80},{3,81},{4,86},{5,87},{6,84},{7,85},{8,90},{9,... | collective-permute-start | bytes 786440 | tf_op jit(solution)/shard_map/ppermute | solution.py:35
  156.9 9.8 %collective-permute-start.35 = (bf16[256,512]{1,0:T(8,128)(2,1)S(1)}, bf16[256,512]{1,0:T(8,128)(2,1)S(1)}, u32[]{:S(2)}, u32[]{:S(2)}) collective-permute-start(bf16[256,512]{1,0:T(8,128)(2,1)S(1)} %shard_map.111.refs_0_.state), channel_id=1, source_target_pairs={{0,4},{1,5},{2,6},{3,7},{4,8},{5,9},{6,10},{7,11},{8,12},{9,13},{1... | collective-permute-start | bytes 786440 | tf_op jit(solution)/shard_map/ppermute | solution.py:35
  157.0 14.5 %collective-permute-start.36 = (bf16[256,512]{1,0:T(8,128)(2,1)S(1)}, bf16[256,512]{1,0:T(8,128)(2,1)S(1)}, u32[]{:S(2)}, u32[]{:S(2)}) collective-permute-start(bf16[256,512]{1,0:T(8,128)(2,1)S(1)} %shard_map.111.refs_0_.state), channel_id=1, source_target_pairs={{0,8},{1,9},{2,10},{3,11},{4,12},{5,13},{6,14},{7,15},{8,0},{9,1},... | collective-permute-start | bytes 786440 | tf_op jit(solution)/shard_map/ppermute | solution.py:35
  160.6 11.1 %collective-permute-start.37 = (bf16[256,512]{1,0:T(8,128)(2,1)S(1)}, bf16[256,512]{1,0:T(8,128)(2,1)S(1)}, u32[]{:S(2)}, u32[]{:S(2)}) collective-permute-start(bf16[256,512]{1,0:T(8,128)(2,1)S(1)} %shard_map.111.refs_0_.state), channel_id=1, source_target_pairs={{0,12},{1,13},{2,14},{3,15},{4,0},{5,1},{6,2},{7,3},{8,4},{9,5},{1... | collective-permute-start | bytes 786440 | tf_op jit(solution)/shard_map/ppermute | solution.py:35
  160.6 11.5 %collective-permute-start.38 = (bf16[256,512]{1,0:T(8,128)(2,1)S(1)}, bf16[256,512]{1,0:T(8,128)(2,1)S(1)}, u32[]{:S(2)}, u32[]{:S(2)}) collective-permute-start(bf16[256,512]{1,0:T(8,128)(2,1)S(1)} %shard_map.111.refs_0_.state), channel_id=1, source_target_pairs={{0,1},{1,0},{2,3},{3,2},{4,5},{5,4},{6,7},{7,6},{8,9},{9,8},{10,11... | collective-permute-start | bytes 786440 | tf_op jit(solution)/shard_map/ppermute | solution.py:35
  184.7 10.8 %collective-permute-start.43 = (bf16[256,512]{1,0:T(8,128)(2,1)S(1)}, bf16[256,512]{1,0:T(8,128)(2,1)S(1)}, u32[]{:S(2)}, u32[]{:S(2)}) collective-permute-start(bf16[256,512]{1,0:T(8,128)(2,1)S(1)} %get-tuple-element.58), channel_id=1, source_target_pairs={{0,8},{1,9},{2,10},{3,11},{4,12},{5,13},{6,14},{7,15},{8,0},{9,1},... | collective-permute-start | bytes 786440 | tf_op jit(solution)/shard_map/ppermute | solution.py:35
  185.4 14.9 %collective-permute-start.44 = (bf16[256,512]{1,0:T(8,128)(2,1)S(1)}, bf16[256,512]{1,0:T(8,128)(2,1)S(1)}, u32[]{:S(2)}, u32[]{:S(2)}) collective-permute-start(bf16[256,512]{1,0:T(8,128)(2,1)S(1)} %get-tuple-element.59), channel_id=1, source_target_pairs={{0,4},{1,5},{2,6},{3,7},{4,8},{5,9},{6,10},{7,11},{8,12},{9,13},{1... | collective-permute-start | bytes 786440 | tf_op jit(solution)/shard_map/ppermute | solution.py:35
  188.0 12.3 %collective-permute-start.45 = (bf16[256,512]{1,0:T(8,128)(2,1)S(1)}, bf16[256,512]{1,0:T(8,128)(2,1)S(1)}, u32[]{:S(2)}, u32[]{:S(2)}) collective-permute-start(bf16[256,512]{1,0:T(8,128)(2,1)S(1)} %get-tuple-element.60), channel_id=1, source_target_pairs={{0,12},{1,13},{2,14},{3,15},{4,0},{5,1},{6,2},{7,3},{8,4},{9,5},{1... | collective-permute-start | bytes 786440 | tf_op jit(solution)/shard_map/ppermute | solution.py:35
  201.0 15.1 %collective-permute-start.46 = (bf16[256,512]{1,0:T(8,128)(2,1)S(1)}, bf16[256,512]{1,0:T(8,128)(2,1)S(1)}, u32[]{:S(2)}, u32[]{:S(2)}) collective-permute-start(bf16[256,512]{1,0:T(8,128)(2,1)S(1)} %shard_map.114), channel_id=1, source_target_pairs={{0,16},{1,17},{2,18},{3,19},{4,20},{5,21},{6,22},{7,23},{8,24},{9,... | collective-permute-start | bytes 786440 | tf_op jit(solution)/shard_map/ppermute | solution.py:35
  201.1 15.0 %collective-permute-start.47 = (bf16[256,512]{1,0:T(8,128)(2,1)S(1)}, bf16[256,512]{1,0:T(8,128)(2,1)S(1)}, u32[]{:S(2)}, u32[]{:S(2)}) collective-permute-start(bf16[256,512]{1,0:T(8,128)(2,1)S(1)} %shard_map.114), channel_id=1, source_target_pairs={{0,82},{1,83},{2,80},{3,81},{4,86},{5,87},{6,84},{7,85},{8,90},{9,... | collective-permute-start | bytes 786440 | tf_op jit(solution)/shard_map/ppermute | solution.py:35
  216.7 9.9 %collective-permute-start.48 = (bf16[256,512]{1,0:T(8,128)(2,1)S(1)}, bf16[256,512]{1,0:T(8,128)(2,1)S(1)}, u32[]{:S(2)}, u32[]{:S(2)}) collective-permute-start(bf16[256,512]{1,0:T(8,128)(2,1)S(1)} %shard_map.115.refs_0_.state), channel_id=1, source_target_pairs={{0,4},{1,5},{2,6},{3,7},{4,8},{5,9},{6,10},{7,11},{8,12},{9,13},{1... | collective-permute-start | bytes 786440 | tf_op jit(solution)/shard_map/ppermute | solution.py:35
  216.8 14.8 %collective-permute-start.49 = (bf16[256,512]{1,0:T(8,128)(2,1)S(1)}, bf16[256,512]{1,0:T(8,128)(2,1)S(1)}, u32[]{:S(2)}, u32[]{:S(2)}) collective-permute-start(bf16[256,512]{1,0:T(8,128)(2,1)S(1)} %shard_map.115.refs_0_.state), channel_id=1, source_target_pairs={{0,8},{1,9},{2,10},{3,11},{4,12},{5,13},{6,14},{7,15},{8,0},{9,1},... | collective-permute-start | bytes 786440 | tf_op jit(solution)/shard_map/ppermute | solution.py:35
  220.6 11.0 %collective-permute-start.50 = (bf16[256,512]{1,0:T(8,128)(2,1)S(1)}, bf16[256,512]{1,0:T(8,128)(2,1)S(1)}, u32[]{:S(2)}, u32[]{:S(2)}) collective-permute-start(bf16[256,512]{1,0:T(8,128)(2,1)S(1)} %shard_map.115.refs_0_.state), channel_id=1, source_target_pairs={{0,12},{1,13},{2,14},{3,15},{4,0},{5,1},{6,2},{7,3},{8,4},{9,5},{1... | collective-permute-start | bytes 786440 | tf_op jit(solution)/shard_map/ppermute | solution.py:35
  220.6 11.5 %collective-permute-start.51 = (bf16[256,512]{1,0:T(8,128)(2,1)S(1)}, bf16[256,512]{1,0:T(8,128)(2,1)S(1)}, u32[]{:S(2)}, u32[]{:S(2)}) collective-permute-start(bf16[256,512]{1,0:T(8,128)(2,1)S(1)} %shard_map.115.refs_0_.state), channel_id=1, source_target_pairs={{0,1},{1,0},{2,3},{3,2},{4,5},{5,4},{6,7},{7,6},{8,9},{9,8},{10,11... | collective-permute-start | bytes 786440 | tf_op jit(solution)/shard_map/ppermute | solution.py:35
  244.9 10.8 %collective-permute-start.56 = (bf16[256,512]{1,0:T(8,128)(2,1)S(1)}, bf16[256,512]{1,0:T(8,128)(2,1)S(1)}, u32[]{:S(2)}, u32[]{:S(2)}) collective-permute-start(bf16[256,512]{1,0:T(8,128)(2,1)S(1)} %get-tuple-element.64), channel_id=1, source_target_pairs={{0,8},{1,9},{2,10},{3,11},{4,12},{5,13},{6,14},{7,15},{8,0},{9,1},... | collective-permute-start | bytes 786440 | tf_op jit(solution)/shard_map/ppermute | solution.py:35
  245.5 14.9 %collective-permute-start.57 = (bf16[256,512]{1,0:T(8,128)(2,1)S(1)}, bf16[256,512]{1,0:T(8,128)(2,1)S(1)}, u32[]{:S(2)}, u32[]{:S(2)}) collective-permute-start(bf16[256,512]{1,0:T(8,128)(2,1)S(1)} %get-tuple-element.65), channel_id=1, source_target_pairs={{0,4},{1,5},{2,6},{3,7},{4,8},{5,9},{6,10},{7,11},{8,12},{9,13},{1... | collective-permute-start | bytes 786440 | tf_op jit(solution)/shard_map/ppermute | solution.py:35
  248.1 12.3 %collective-permute-start.58 = (bf16[256,512]{1,0:T(8,128)(2,1)S(1)}, bf16[256,512]{1,0:T(8,128)(2,1)S(1)}, u32[]{:S(2)}, u32[]{:S(2)}) collective-permute-start(bf16[256,512]{1,0:T(8,128)(2,1)S(1)} %get-tuple-element.66), channel_id=1, source_target_pairs={{0,12},{1,13},{2,14},{3,15},{4,0},{5,1},{6,2},{7,3},{8,4},{9,5},{1... | collective-permute-start | bytes 786440 | tf_op jit(solution)/shard_map/ppermute | solution.py:35
  261.2 15.1 %collective-permute-start.59 = (bf16[256,512]{1,0:T(8,128)(2,1)S(1)}, bf16[256,512]{1,0:T(8,128)(2,1)S(1)}, u32[]{:S(2)}, u32[]{:S(2)}) collective-permute-start(bf16[256,512]{1,0:T(8,128)(2,1)S(1)} %shard_map.118), channel_id=1, source_target_pairs={{0,16},{1,17},{2,18},{3,19},{4,20},{5,21},{6,22},{7,23},{8,24},{9,... | collective-permute-start | bytes 786440 | tf_op jit(solution)/shard_map/ppermute | solution.py:35
  261.2 15.0 %collective-permute-start.60 = (bf16[256,512]{1,0:T(8,128)(2,1)S(1)}, bf16[256,512]{1,0:T(8,128)(2,1)S(1)}, u32[]{:S(2)}, u32[]{:S(2)}) collective-permute-start(bf16[256,512]{1,0:T(8,128)(2,1)S(1)} %shard_map.118), channel_id=1, source_target_pairs={{0,82},{1,83},{2,80},{3,81},{4,86},{5,87},{6,84},{7,85},{8,90},{9,... | collective-permute-start | bytes 786440 | tf_op jit(solution)/shard_map/ppermute | solution.py:35
  276.9 9.9 %collective-permute-start.61 = (bf16[256,512]{1,0:T(8,128)(2,1)S(1)}, bf16[256,512]{1,0:T(8,128)(2,1)S(1)}, u32[]{:S(2)}, u32[]{:S(2)}) collective-permute-start(bf16[256,512]{1,0:T(8,128)(2,1)S(1)} %shard_map.119.refs_0_), channel_id=1, source_target_pairs={{0,4},{1,5},{2,6},{3,7},{4,8},{5,9},{6,10},{7,11},{8,12},{9,13},{1... | collective-permute-start | bytes 786440 | tf_op jit(solution)/shard_map/ppermute | solution.py:35
  277.0 14.7 %collective-permute-start.62 = (bf16[256,512]{1,0:T(8,128)(2,1)S(1)}, bf16[256,512]{1,0:T(8,128)(2,1)S(1)}, u32[]{:S(2)}, u32[]{:S(2)}) collective-permute-start(bf16[256,512]{1,0:T(8,128)(2,1)S(1)} %shard_map.119.refs_0_), channel_id=1, source_target_pairs={{0,8},{1,9},{2,10},{3,11},{4,12},{5,13},{6,14},{7,15},{8,0},{9,1},... | collective-permute-start | bytes 786440 | tf_op jit(solution)/shard_map/ppermute | solution.py:35
  280.7 11.0 %collective-permute-start.63 = (bf16[256,512]{1,0:T(8,128)(2,1)S(1)}, bf16[256,512]{1,0:T(8,128)(2,1)S(1)}, u32[]{:S(2)}, u32[]{:S(2)}) collective-permute-start(bf16[256,512]{1,0:T(8,128)(2,1)S(1)} %shard_map.119.refs_0_), channel_id=1, source_target_pairs={{0,12},{1,13},{2,14},{3,15},{4,0},{5,1},{6,2},{7,3},{8,4},{9,5},{1... | collective-permute-start | bytes 786440 | tf_op jit(solution)/shard_map/ppermute | solution.py:35
  280.7 11.5 %collective-permute-start.64 = (bf16[256,512]{1,0:T(8,128)(2,1)S(1)}, bf16[256,512]{1,0:T(8,128)(2,1)S(1)}, u32[]{:S(2)}, u32[]{:S(2)}) collective-permute-start(bf16[256,512]{1,0:T(8,128)(2,1)S(1)} %shard_map.119.refs_0_), channel_id=1, source_target_pairs={{0,1},{1,0},{2,3},{3,2},{4,5},{5,4},{6,7},{7,6},{8,9},{9,8},{10,11... | collective-permute-start | bytes 786440 | tf_op jit(solution)/shard_map/ppermute | solution.py:35
  303.0 14.4 %all-to-all-start = ((f32[16,16,256]{2,1,0:T(8,128)}), f32[16,16,256]{2,1,0:T(8,128)S(1)}, u32[]{:S(2)}, u32[]{:S(2)}) async-start(f32[16,16,256]{2,1,0:T(8,128)} %get-tuple-element.71), calls=%async_computation | async-start | bytes 524288 | tf_op jit(solution)/shard_map/all_to_all | solution.py:476
  318.2 12.8 %all-to-all-start.1 = ((bf16[32,16,256]{2,1,0:T(8,128)(2,1)}), bf16[32,16,256]{2,1,0:T(8,128)(2,1)S(1)}, u32[]{:S(2)}, u32[]{:S(2)}) async-start(bf16[32,16,256]{2,1,0:T(8,128)(2,1)} %broadcast_in_dim.6), calls=%async_computation.1 | async-start | bytes 524288 | tf_op jit(solution)/shard_map/all_to_all | solution.py:483
  (29 other events, 155.2 us)
